TPU v7x, 256 devices: a whole 4x4x8 slice. The times are simulated.
256 devices in a mesh: dp: 16 (over x, y), mp: 16 (over z, core).
Axes of the slice: x: 4, y: 4, z: 8, core: 2. Of those that a mesh axis runs over, the one named last changes fastest.
Arguments:
- hidden_in: bfloat16 [2048, 4096], P('dp', 'mp'), may hold values from -6 to 6
- lengths: int32 [16], P('dp'), may hold values from 1 to 128
- norm_attn: float32 [4096], replicated, may hold values from 0.25 to 1.75
- q_weight: bfloat16 [4096, 4096], P('dp', 'mp'), may hold values from -0.01171875 to 0.01171875
- k_weight: bfloat16 [4096, 4096], P('dp', 'mp'), may hold values from -0.09375 to 0.09375
- v_weight: bfloat16 [4096, 4096], P('dp', 'mp'), may hold values from -0.09375 to 0.09375
- out_weight_t: bfloat16 [4096, 4096], P('dp', 'mp'), may hold values from -0.09375 to 0.09375
- norm_ffn: float32 [4096], replicated, may hold values from 0.25 to 1.75
- gate_weight: bfloat16 [4096, 10240], P('dp', 'mp'), may hold values from -0.09375 to 0.09375
- up_weight: bfloat16 [4096, 10240], P('dp', 'mp'), may hold values from -0.09375 to 0.09375
- down_weight_t: bfloat16 [4096, 10240], P('dp', 'mp'), may hold values from -0.0625 to 0.0625
- scale_key: float32 [4096], P('mp'), may hold values from 0.25 to 4
- scale_value: float32 [4096], P('mp'), may hold values from 0.1 to 1.9
- scale_ffn: float32 [10240], P('mp'), may hold values from 0.1 to 1.9
- out_grad: bfloat16 [2048, 4096], P('dp'), may hold values from -6 to 6
- position_bias: float32 [64, 128, 128], P('mp'), may hold values from -6 to 256
Outputs:
- block_out: bfloat16 [2048, 4096], P('dp', 'mp')
- input_grad: bfloat16 [2048, 4096], P('dp', 'mp')
- grad_key: float32 [4096], P('mp')
- grad_value: float32 [4096], P('mp')
- grad_ffn: float32 [10240], P('mp')
Inputs may be any that keep to these rules, and one draw needn't show every extreme that they name: Keys of sequence b at positions lengths[b] and beyond are padding.
All inputs are finite; a program needn't handle non-finite values.
Results may differ from a plain program's by a relative error of at most 0.03.
Values may be sent and summed in bfloat16 or wider, within the bound.
A program may use at most 128 MiB of HBM per device.

v0:
```python
import functools

import jax
import jax.numpy as jnp
from jax import lax
from jax.sharding import Mesh
from jax.sharding import PartitionSpec as P

HEAD_DIM = 64
MP = ("mp_0", "mp_1")
DP = ("dp_0", "dp_1")


EPSILON = 1e-06
NEGATIVE = -1e30


def side_by_side(arrays, axis, dim, along):
    ends, at = ([], 0)
    for a in arrays[:-1]:
        at += a.shape[along]
        ends.append(at)
    both = jnp.concatenate(arrays, axis=along)
    return tuple(jnp.split(lax.all_gather(both, axis, axis=dim, tiled=True), ends, axis=along))


def in_blocks(x, dim, devices):
    dims = x.shape
    blocks = x.reshape(*dims[:dim], devices, dims[dim] // devices, *dims[dim + 1 :])
    return jnp.moveaxis(blocks, dim, 0)


def summed_on_arrival(x, axis, dim):
    blocks = in_blocks(x, dim, lax.axis_size(axis))
    arrived = lax.all_to_all(blocks, axis, split_axis=0, concat_axis=0, tiled=True)
    return arrived.astype(jnp.float32).sum(axis=0)


def summed_rows(x, axes, dim):
    far, near = axes
    blocks = in_blocks(x, dim, lax.axis_size(far))
    nearer = summed_on_arrival(blocks, near, dim + 1)
    arrived = lax.all_to_all(
        nearer.astype(jnp.bfloat16), far, split_axis=0, concat_axis=0, tiled=True
    )
    return arrived.astype(jnp.float32).sum(axis=0)


def filled_up(lines, devices):
    spare = -len(lines) % devices
    return jnp.pad(lines, [(0, spare)] + [(0, 0)] * (lines.ndim - 1))


def from_everyone(x, axis):
    copies = jnp.broadcast_to(x, (lax.axis_size(axis), *x.shape))
    return lax.all_to_all(copies, axis, split_axis=0, concat_axis=0, tiled=True)


def laid_out(blocks, dim):
    dims = list(blocks.shape[1:])
    dims[dim] *= blocks.shape[0]
    return jnp.moveaxis(blocks, 0, dim).reshape(dims)


def gather_axes(x, axes, dim):
    far, near = axes
    blocks = from_everyone(from_everyone(x, far), near)
    return laid_out(blocks.swapaxes(0, 1).reshape(-1, *x.shape), dim)


def sum_by_parts(x, axes):
    lines = x.reshape(-1, x.shape[-1])
    own = summed_rows(filled_up(lines, lax.axis_size(axes[0]) * lax.axis_size(axes[1])), axes, 0)
    whole = gather_axes(own.astype(jnp.bfloat16), axes, 0)
    return whole[: len(lines)].reshape(x.shape).astype(jnp.float32)


def of_everyone(x, axis):
    everything = from_everyone(x, axis)
    return jnp.sum(everything, axis=0)


def over_axes(x, axes):
    return functools.reduce(lax.psum, axes, x)


def inverse_rms(values):
    return lax.rsqrt(jnp.mean(values * values, axis=-1, keepdims=True) + EPSILON)


def gelu_tanh(values):
    return jax.nn.gelu(values, approximate=True)


def contract_last(left_side, right_side):
    return lax.dot_general(
        left_side, right_side, (((1,), (1,)), ((), ())), preferred_element_type=jnp.float32
    )


def norm_back(grad_in, values, inverse, gain_vec):
    scaled = grad_in * gain_vec
    correction = (
        values * inverse * inverse * inverse * jnp.mean(scaled * values, axis=-1, keepdims=True)
    )
    return inverse * scaled - correction


def on_device(
    hidden_in,
    lengths,
    norm_attn,
    q_weight,
    k_weight,
    v_weight,
    out_weight_t,
    norm_ffn,
    gate_weight,
    up_weight,
    down_weight_t,
    scale_key,
    scale_value,
    scale_ffn,
    out_grad,
    position_bias,
):
    full_inputs = lax.all_gather(hidden_in, MP, axis=1, tiled=True)
    q_full, k_full, v_full, o_full, gate_full, up_full, down_full = side_by_side(
        (q_weight, k_weight, v_weight, out_weight_t, gate_weight, up_weight, down_weight_t),
        DP,
        0,
        1,
    )
    seq_local = lengths.shape[0]
    tokens_local = full_inputs.shape[0]
    seq_len = tokens_local // seq_local
    heads_local = q_full.shape[1] // HEAD_DIM
    shaped = (seq_local, seq_len, heads_local, HEAD_DIM)
    inputs32 = full_inputs.astype(jnp.float32)
    inv_first = inverse_rms(inputs32)
    normed_first = (inputs32 * inv_first * norm_attn).astype(jnp.bfloat16)
    queries = jnp.dot(normed_first, q_full, preferred_element_type=jnp.float32).astype(jnp.bfloat16)
    key_pre = jnp.dot(normed_first, k_full, preferred_element_type=jnp.float32)
    value_pre = jnp.dot(normed_first, v_full, preferred_element_type=jnp.float32)
    key_rows = (key_pre * scale_key).astype(jnp.bfloat16)
    value_rows = (value_pre * scale_value).astype(jnp.bfloat16)
    q_heads = queries.reshape(shaped)
    k_heads = key_rows.reshape(shaped)
    v_heads = value_rows.reshape(shaped)
    scores = (
        jnp.einsum("bihe,bjhe->bhij", q_heads, k_heads, preferred_element_type=jnp.float32)
        + position_bias[None]
    )
    positions = lax.broadcasted_iota(jnp.int32, (seq_local, seq_len), 1)
    valid_keys = positions < lengths[:, None]
    scores = jnp.where(valid_keys[:, None, None, :], scores, NEGATIVE)
    largest = jnp.max(scores, axis=-1, keepdims=True)
    exponent = jnp.exp(scores - largest)
    attn_probs = exponent / jnp.sum(exponent, axis=-1, keepdims=True)
    probs_low = attn_probs.astype(jnp.bfloat16)
    context = (
        jnp.einsum("bhij,bjhe->bihe", probs_low, v_heads, preferred_element_type=jnp.float32)
        .reshape(tokens_local, -1)
        .astype(jnp.bfloat16)
    )
    attended = sum_by_parts(contract_last(context, o_full).astype(jnp.bfloat16), ("mp_0", "mp_1"))
    first_sum = inputs32 + attended
    inv_second = inverse_rms(first_sum)
    normed_second = (first_sum * inv_second * norm_ffn).astype(jnp.bfloat16)
    gate_proj = jnp.dot(normed_second, gate_full, preferred_element_type=jnp.float32)
    upward = jnp.dot(normed_second, up_full, preferred_element_type=jnp.float32)
    activated, gelu_back = jax.vjp(gelu_tanh, gate_proj)
    product = activated * upward
    hidden = (product * scale_ffn).astype(jnp.bfloat16)
    ffn_share = summed_on_arrival(contract_last(hidden, down_full).astype(jnp.bfloat16), MP, 1)
    share_width = ffn_share.shape[1]
    offset = lax.axis_index(MP) * share_width
    first_share = lax.dynamic_slice_in_dim(first_sum, offset, share_width, 1)
    block_out = (first_share + ffn_share).astype(jnp.bfloat16)
    d_hidden = jnp.dot(out_grad, down_full, preferred_element_type=jnp.float32)
    grad_ffn_part = jnp.sum(d_hidden * product, axis=0)
    d_product = d_hidden * scale_ffn
    d_gate = gelu_back(d_product * upward)[0].astype(jnp.bfloat16)
    d_up = (d_product * activated).astype(jnp.bfloat16)
    d_second = sum_by_parts(
        (contract_last(d_gate, gate_full) + contract_last(d_up, up_full)).astype(jnp.bfloat16),
        ("mp_0", "mp_1"),
    )
    d_first = out_grad.astype(jnp.float32) + norm_back(d_second, first_sum, inv_second, norm_ffn)
    d_context = jnp.dot(
        d_first.astype(jnp.bfloat16), o_full, preferred_element_type=jnp.float32
    ).astype(jnp.bfloat16)
    dc_heads = d_context.reshape(shaped)
    d_probs = jnp.einsum("bihe,bjhe->bhij", dc_heads, v_heads, preferred_element_type=jnp.float32)
    d_scores = (
        attn_probs * (d_probs - jnp.sum(attn_probs * d_probs, axis=-1, keepdims=True))
    ).astype(jnp.bfloat16)
    d_values = jnp.einsum(
        "bhij,bihe->bjhe", probs_low, dc_heads, preferred_element_type=jnp.float32
    ).reshape(tokens_local, -1)
    d_keys = jnp.einsum(
        "bhij,bihe->bjhe", d_scores, q_heads, preferred_element_type=jnp.float32
    ).reshape(tokens_local, -1)
    d_queries = (
        jnp.einsum("bhij,bjhe->bihe", d_scores, k_heads, preferred_element_type=jnp.float32)
        .reshape(tokens_local, -1)
        .astype(jnp.bfloat16)
    )
    grad_key_part = jnp.sum(d_keys * key_pre, axis=0)
    grad_value_part = jnp.sum(d_values * value_pre, axis=0)
    d_key_pre = (d_keys * scale_key).astype(jnp.bfloat16)
    d_value_pre = (d_values * scale_value).astype(jnp.bfloat16)
    attn_term = (
        contract_last(d_queries, q_full)
        + contract_last(d_key_pre, k_full)
        + contract_last(d_value_pre, v_full)
    )
    d_share = summed_on_arrival(attn_term.astype(jnp.bfloat16), MP, 1)
    gain_share = lax.dynamic_slice_in_dim(norm_attn, offset, share_width, 0)
    input_share = lax.dynamic_slice_in_dim(inputs32, offset, share_width, 1)
    first_grad_share = lax.dynamic_slice_in_dim(d_first, offset, share_width, 1)
    scaled_grad = d_share * gain_share
    dot_share = jnp.sum(scaled_grad * input_share, axis=-1, keepdims=True)
    dot_total = of_everyone(dot_share, MP)
    mean_dot = dot_total / inputs32.shape[1]
    cubed = inv_first * inv_first * inv_first
    input_grad = (
        first_grad_share + inv_first * scaled_grad - input_share * cubed * mean_dot
    ).astype(jnp.bfloat16)
    grad_key, grad_value, grad_ffn = (
        over_axes(grad_key_part, DP),
        over_axes(grad_value_part, DP),
        over_axes(grad_ffn_part, DP),
    )
    return (block_out, input_grad, grad_key, grad_value, grad_ffn)


def solution(mesh):
    finer = Mesh(mesh.devices.reshape(4, 4, 8, 2), ("dp_0", "dp_1", "mp_0", "mp_1"))
    placed = (
        P(DP, MP),
        P(DP),
        P(),
        P(DP, MP),
        P(DP, MP),
        P(DP, MP),
        P(DP, MP),
        P(),
        P(DP, MP),
        P(DP, MP),
        P(DP, MP),
        P(MP),
        P(MP),
        P(MP),
        P(DP, None),
        P(MP, None, None),
    )
    return jax.shard_map(
        on_device,
        mesh=finer,
        in_specs=placed,
        out_specs=(P(DP, MP), P(DP, MP), P(MP), P(MP), P(MP)),
        check_vma=False,
    )
```

profile of v0, /device:TPU:33, one launch (start us, length us, event | category | flops | bytes accessed | tf_op | source)
XLA Modules:
  0.0 435.8 jit_solution(16360203652515288852)
XLA Ops:
  13.8 1.2 copy-done.3
  15.9 34.0 %all-gather.3.cloned.1.call-done = bf16[128,4096]{1,0:T(8,128)(2,1)} async-done(((bf16[128,256]{1,0:T(8,128)(2,1)}), bf16[128,4096]{1,0:T(8,128)(2,1)}) %all-gather.3.cloned.1.call-update) | async-done | bytes 1048592 | tf_op jit(solution)/shard_map/all_gather | solution.py:127
  49.9 1.5 multiply_reduce_fusion.2
  51.9 153.0 %all-gather.5.cloned.1.call-done = bf16[4096,2944]{1,0:T(8,128)(2,1)} async-done(((bf16[256,2944]{1,0:T(8,128)(2,1)}), bf16[4096,2944]{1,0:T(8,128)(2,1)}) %all-gather.5.cloned.1.call-update) | async-done | bytes 24117264 | tf_op jit(solution)/shard_map/all_gather | solution.py:24
  204.9 3.1 multiply_convert_fusion.10
  208.2 2.1 fusion.32
  210.4 2.7 multiply_convert_fusion.9
  214.3 2.4 convolution_convert_fusion.1
  216.8 5.0 %all_to_all.55 = bf16[2,8,8,4096]{3,2,1,0:T(8,128)(2,1)S(1)} all-to-all(bf16[2,8,8,4096]{3,2,1,0:T(8,128)(2,1)S(1)} %bitcast.82), channel_id=1, replica_groups=mesh['dp_0'=4,'dp_1'=4,'mp_0'=8,'mp_1'=2] {'mp_1'}, dimensions={0} | all-to-all | bytes 2097152 | tf_op jit(solution)/shard_map/all_to_all | solution.py:35
  222.2 21.1 %all_to_all.56 = bf16[8,8,4096]{2,1,0:T(8,128)(2,1)S(1)} all-to-all(bf16[8,8,4096]{2,1,0:T(8,128)(2,1)S(1)} %reduce_sum.158), channel_id=1, replica_groups=mesh['dp_0'=4,'dp_1'=4,'mp_0'=8,'mp_1'=2] {'mp_0'}, dimensions={0} | all-to-all | bytes 1048576 | tf_op jit(solution)/shard_map/all_to_all | solution.py:43
  243.4 18.5 %all_to_all.57 = bf16[8,8,4096]{2,1,0:T(8,128)(2,1)S(1)} all-to-all(bf16[8,8,4096]{2,1,0:T(8,128)(2,1)S(1)} %broadcast_in_dim.24), channel_id=1, replica_groups=mesh['dp_0'=4,'dp_1'=4,'mp_0'=8,'mp_1'=2] {'mp_0'}, dimensions={0} | all-to-all | bytes 1048576 | tf_op jit(solution)/shard_map/all_to_all | solution.py:56
  262.0 7.8 %all_to_all.58 = bf16[2,8,8,4096]{3,2,1,0:T(8,128)(2,1)S(1)} all-to-all(bf16[2,8,8,4096]{3,2,1,0:T(8,128)(2,1)S(1)} %broadcast_in_dim.25), channel_id=1, replica_groups=mesh['dp_0'=4,'dp_1'=4,'mp_0'=8,'mp_1'=2] {'mp_1'}, dimensions={0} | all-to-all | bytes 2097152 | tf_op jit(solution)/shard_map/all_to_all | solution.py:56
  270.7 3.5 fusion.7
  274.3 3.7 fusion.11
  278.0 3.7 multiply_reduce_fusion.3
  281.6 4.3 fusion.9
  286.0 4.3 fusion.1
  290.4 5.4 %all_to_all.59 = bf16[2,8,8,4096]{3,2,1,0:T(8,128)(2,1)} all-to-all(bf16[2,8,8,4096]{3,2,1,0:T(8,128)(2,1)S(1)} %bitcast.83), channel_id=1, replica_groups=mesh['dp_0'=4,'dp_1'=4,'mp_0'=8,'mp_1'=2] {'mp_1'}, dimensions={0} | all-to-all | bytes 2097152 | tf_op jit(solution)/shard_map/all_to_all | solution.py:35
  295.7 2.4 reduce_sum.162
  298.1 20.6 %all_to_all.60 = bf16[8,8,4096]{2,1,0:T(8,128)(2,1)} all-to-all(bf16[8,8,4096]{2,1,0:T(8,128)(2,1)} %reduce_sum.162), channel_id=1, replica_groups=mesh['dp_0'=4,'dp_1'=4,'mp_0'=8,'mp_1'=2] {'mp_0'}, dimensions={0} | all-to-all | bytes 1048576 | tf_op jit(solution)/shard_map/all_to_all | solution.py:43
  318.7 1.1 reduce_sum.163
  320.7 6.7 %all-to-all-start.7 = ((bf16[8,8,4096]{2,1,0:T(8,128)(2,1)}), bf16[8,8,4096]{2,1,0:T(8,128)(2,1)}, u32[]{:S(2)}, u32[]{:S(2)}) async-start(bf16[8,8,4096]{2,1,0:T(8,128)(2,1)} %broadcast_in_dim.26), calls=%async_computation.7 | async-start | bytes 1048576 | tf_op jit(solution)/shard_map/all_to_all | solution.py:56
  327.4 4.5 %convolution_convert_fusion = bf16[128,4096]{1,0:T(8,128)(2,1)S(1)} fusion(bf16[4096,2944]{1,0:T(8,128)(2,1)} %all-gather.5.cloned.1.call-done, f32[640]{0:T(1024)S(1)} %copy-done.17, f32[128,640]{1,0:T(8,128)} %copy-done.24, f32[128,640]{1,0:T(8,128)} %copy-done.9), kind=kOutput, calls=%fused_computation.6 | convolution fusion | flops 672514048 | bytes 6949376 | tf_op jit(solution)/shard_map/dot_general | solution.py:96
  331.8 1.1 copy.118
  332.9 10.3 %all-to-all-done.7 = bf16[8,8,4096]{2,1,0:T(8,128)(2,1)} async-done(((bf16[8,8,4096]{2,1,0:T(8,128)(2,1)}), bf16[8,8,4096]{2,1,0:T(8,128)(2,1)}, u32[]{:S(2)}, u32[]{:S(2)}) %all-to-all-start.7) | async-done | bytes 524320 | tf_op jit(solution)/shard_map/all_to_all | solution.py:56
  343.3 1.1 broadcast_in_dim.27
  344.4 6.5 %all_to_all.61 = bf16[2,8,8,4096]{3,2,1,0:T(8,128)(2,1)} all-to-all(bf16[2,8,8,4096]{3,2,1,0:T(8,128)(2,1)S(1)} %broadcast_in_dim.27), channel_id=1, replica_groups=mesh['dp_0'=4,'dp_1'=4,'mp_0'=8,'mp_1'=2] {'mp_1'}, dimensions={0} | all-to-all | bytes 2097152 | tf_op jit(solution)/shard_map/all_to_all | solution.py:56
  350.9 4.2 all-to-all-start.4
  355.2 1.7 multiply_reduce_fusion
  357.8 1.4 copy-done.2
  359.1 2.1 fusion.35
  362.0 1.1 multiply_reduce_fusion.4
  364.3 1.9 fusion.57
  368.2 2.4 fusion.19
  370.6 2.4 convolution_add_fusion.1
  373.1 2.5 fusion.2
  375.5 1.1 copy.117
  376.6 3.5 all-to-all-done.4
  380.1 6.6 %all-to-all-start.9 = ((bf16[16,128,256]{2,1,0:T(8,128)(2,1)}), bf16[16,128,256]{2,1,0:T(8,128)(2,1)}, u32[]{:S(2)}, u32[]{:S(2)}) async-start(bf16[16,128,256]{2,1,0:T(8,128)(2,1)} %bitcast.80), calls=%async_computation.9 | async-start | bytes 2097152 | tf_op jit(solution)/shard_map/all_to_all | solution.py:35
  387.5 1.6 convert_element_type.124
  389.2 9.3 %all-reduce.1 = (f32[256]{0:T(256)S(1)}, f32[256]{0:T(256)S(1)}, f32[640]{0:T(1024)S(1)}) all-reduce(f32[256]{0:T(256)S(1)} %get-tuple-element.26, f32[256]{0:T(256)S(1)} %get-tuple-element.25, f32[640]{0:T(1024)S(1)} %get-tuple-element.23), channel_id=1, replica_groups=mesh['dp_0'=4,'dp_1'=4,'mp_0'=8,'mp_1'=2] {'dp_0'}, use_global_device_ids=true, to_apply=%region_15.16 | all-reduce | flops 1152 | bytes 9216 | tf_op jit(solution)/shard_map/psum | solution.py:84
  398.5 8.1 %all-reduce = (f32[256]{0:T(256)}, f32[256]{0:T(256)}, f32[640]{0:T(1024)}) all-reduce(f32[256]{0:T(256)S(1)} %get-tuple-element.8, f32[256]{0:T(256)S(1)} %get-tuple-element.9, f32[640]{0:T(1024)S(1)} %get-tuple-element.10), channel_id=1, replica_groups=mesh['dp_0'=4,'dp_1'=4,'mp_0'=8,'mp_1'=2] {'dp_1'}, use_global_device_ids=true, to_apply=%region_16.17 | all-reduce | flops 1152 | bytes 9216 | tf_op jit(solution)/shard_map/psum | solution.py:84
  406.5 1.4 convert_reduce_fusion.1
  407.9 3.8 all-to-all-done.9
  411.7 1.4 convert_reduce_fusion
  414.7 6.5 %all-to-all-start.10 = ((f32[16,128,1]{1,2,0:T(1,128)}), f32[16,128,1]{1,2,0:T(1,128)S(1)}, u32[]{:S(2)}, u32[]{:S(2)}) async-start(f32[16,128,1]{1,2,0:T(1,128)} %broadcast_in_dim.28), calls=%async_computation.10 | async-start | bytes 16384 | tf_op jit(solution)/shard_map/all_to_all | solution.py:56
  421.9 5.3 %all-to-all-done.10 = f32[16,128,1]{1,2,0:T(1,128)S(1)} async-done(((f32[16,128,1]{1,2,0:T(1,128)}), f32[16,128,1]{1,2,0:T(1,128)S(1)}, u32[]{:S(2)}, u32[]{:S(2)}) %all-to-all-start.10) | async-done | bytes 8224 | tf_op jit(solution)/shard_map/all_to_all | solution.py:56
  427.2 1.7 subtract_convert_fusion
  (93 shorter events, 18.9 us)
Async XLA Ops:
  7.2 6.6 %copy-start.10 = (bf16[256,640]{1,0:T(8,128)(2,1)S(1)}, bf16[256,640]{1,0:T(8,128)(2,1)}, u32[]{:S(2)}) copy-start(bf16[256,640]{1,0:T(8,128)(2,1)} %param.26) | copy-start | bytes 983044
  7.2 42.7 %all-gather.3.cloned.1.call-start = ((), (), s32[]{:S(2)}) async-start(), calls=%async_computation.11 | async-start | bytes 1114112 | tf_op jit(solution)/shard_map/all_gather | solution.py:127
  7.9 197.0 %all-gather.5.cloned.1.call-start = ((), (), s32[]{:S(2)}) async-start(), calls=%async_computation.12 | async-start | bytes 25624576 | tf_op jit(solution)/shard_map/all_gather | solution.py:24
  8.9 6.2 %copy-start.11 = (f32[4,128,128]{2,1,0:T(8,128)S(1)}, f32[4,128,128]{2,1,0:T(8,128)}, u32[]{:S(2)}) copy-start(f32[4,128,128]{2,1,0:T(8,128)} %param.31) | copy-start | bytes 786436
  12.7 192.2 %copy-start.18 = (f32[256]{0:T(256)S(1)}, f32[256]{0:T(256)}, u32[]{:S(2)}) copy-start(f32[256]{0:T(256)} %param.28) | copy-start | bytes 3076
  12.7 192.2 %copy-start.23 = (f32[4096]{0:T(1024)S(1)}, f32[4096]{0:T(1024)}, u32[]{:S(2)}) copy-start(f32[4096]{0:T(1024)} %param.18) | copy-start | bytes 49156
  13.8 1.2 copy-start.3
  51.9 158.5 %copy-start.21 = (f32[128]{0:T(128)}, f32[128]{0:T(128)S(1)}, u32[]{:S(2)}) copy-start(f32[128]{0:T(128)S(1)} %get-tuple-element.14) | copy-start | bytes 1540
  204.9 3.3 copy-start
  208.2 5.7 %copy-start.15 = (bf16[128,256]{0,1:T(8,128)(2,1)}, bf16[128,256]{0,1:T(8,128)(2,1)S(1)}, u32[]{:S(2)}) copy-start(bf16[128,256]{0,1:T(8,128)(2,1)S(1)} %copy.85) | copy-start | bytes 196612
  208.2 2.2 copy-start.19
  210.4 2.9 copy-start.7
  213.3 0.8 copy-start.8
  213.6 0.7 copy-start.4
  270.0 0.7 copy-start.14
  274.2 7.4 %copy-start.24 = (f32[128,640]{1,0:T(8,128)}, f32[128,640]{1,0:T(8,128)S(1)}, u32[]{:S(2)}) copy-start(f32[128,640]{1,0:T(8,128)S(1)} %fusion.7) | copy-start | bytes 983044
  274.2 3.7 copy-start.5
  277.9 8.0 %copy-start.9 = (f32[128,640]{1,0:T(8,128)}, f32[128,640]{1,0:T(8,128)S(1)}, u32[]{:S(2)}) copy-start(f32[128,640]{1,0:T(8,128)S(1)} %fusion.11) | copy-start | bytes 983044
  277.9 3.7 copy-start.17
  320.7 22.6 %all-to-all-start.7 = ((bf16[8,8,4096]{2,1,0:T(8,128)(2,1)}), bf16[8,8,4096]{2,1,0:T(8,128)(2,1)}, u32[]{:S(2)}, u32[]{:S(2)}) async-start(bf16[8,8,4096]{2,1,0:T(8,128)(2,1)} %broadcast_in_dim.26), calls=%async_computation.7 | async-start | bytes 1048576 | tf_op jit(solution)/shard_map/all_to_all | solution.py:56
  350.9 29.2 %all-to-all-start.4 = ((bf16[16,128,256]{2,1,0:T(8,128)(2,1)}), bf16[16,128,256]{2,1,0:T(8,128)(2,1)}, u32[]{:S(2)}, u32[]{:S(2)}) async-start(bf16[16,128,256]{2,1,0:T(8,128)(2,1)} %bitcast.81), calls=%async_computation.4 | async-start | bytes 2097152 | tf_op jit(solution)/shard_map/all_to_all | solution.py:35
  355.1 1.8 copy-start.1
  355.1 1.8 copy-start.6
  357.7 1.4 copy-start.2
  359.1 2.8 copy-start.16
  380.1 31.6 %all-to-all-start.9 = ((bf16[16,128,256]{2,1,0:T(8,128)(2,1)}), bf16[16,128,256]{2,1,0:T(8,128)(2,1)}, u32[]{:S(2)}, u32[]{:S(2)}) async-start(bf16[16,128,256]{2,1,0:T(8,128)(2,1)} %bitcast.80), calls=%async_computation.9 | async-start | bytes 2097152 | tf_op jit(solution)/shard_map/all_to_all | solution.py:35
  386.7 2.4 copy-start.12
  386.7 2.4 copy-start.13
  389.1 38.1 %copy-start.20 = (f32[128]{0:T(128)S(1)}, f32[128]{0:T(128)}, u32[]{:S(2)}) copy-start(f32[128]{0:T(128)} %get-tuple-element.13) | copy-start | bytes 1540
  389.1 38.1 %copy-start.22 = (f32[128]{0:T(128)S(1)}, f32[128]{0:T(128)}, u32[]{:S(2)}) copy-start(f32[128]{0:T(128)} %copy-done.21) | copy-start | bytes 1540
  414.7 12.4 %all-to-all-start.10 = ((f32[16,128,1]{1,2,0:T(1,128)}), f32[16,128,1]{1,2,0:T(1,128)S(1)}, u32[]{:S(2)}, u32[]{:S(2)}) async-start(f32[16,128,1]{1,2,0:T(1,128)} %broadcast_in_dim.28), calls=%async_computation.10 | async-start | bytes 16384 | tf_op jit(solution)/shard_map/all_to_all | solution.py:56
Sparse Core Ops, SparseCore 0:
  9.7 40.1 all-gather.2
  52.4 152.4 all-gather.4
where the time goes:
time: 440 us; the launch traced here: 436 us
  waiting for transfers between devices  211 us (48%)
  blocking collectives  102 us (23%)
  matrix products  49.2 us (11%)
  starting transfers between devices  24.1 us (5%)
  local copies, waits for them, and re-layouts  17.2 us (4%)
  other arithmetic  17.2 us (4%)
  between operations  15.3 us (3%)
    all_gather x1, waiting for transfers between devices, side_by_side(): lax.all_gather(both, axis, axis=dim, tiled=True)  153 us
    all_to_all x2, blocking collectives, summed_rows(): lax.all_to_all(nearer.astype(jnp.bfloat16), far, split_axis=0, concat_axi...  41.6 us
    all_gather x1, waiting for transfers between devices, on_device(): full_inputs = lax.all_gather(hidden_in, MP, axis=1, tiled=True)  34 us
    all_to_all x3, blocking collectives, from_everyone(): return lax.all_to_all(copies, axis, split_axis=0, concat_axis=0, tiled=True)  32.8 us
    dot_general x7, matrix products, contract_last(): lax.dot_general(left_side, right_side, (((1,), (1,)), ((), ())), preferre...  22.8 us
    psum x2, blocking collectives, over_axes(): return functools.reduce(lax.psum, axes, x)  17.4 us
    all_to_all x2, waiting for transfers between devices, from_everyone(): return lax.all_to_all(copies, axis, split_axis=0, concat_axis=0, tiled=True)  15.6 us
    all_to_all x2, starting transfers between devices, from_everyone(): return lax.all_to_all(copies, axis, split_axis=0, concat_axis=0, tiled=True)  13.2 us
  transfers between devices with their start and end apart: 6, of which 6 were waited for; matrix products, arithmetic and copies ran while one was open for 9% of the time, Pallas kernels for 0%

commit v1 on v0

v1 whole, which is shorter than its diff:
```python
import functools
import math

import jax
import jax.numpy as jnp
from jax import lax
from jax.experimental import pallas as pl
from jax.experimental.pallas import tpu as pltpu
from jax.sharding import Mesh
from jax.sharding import PartitionSpec as P

HEAD_DIM = 64
EPSILON = 1e-06
NEGATIVE = -1e30
XA, YA, ZA, CA = "dp_0", "dp_1", "mp_0", "mp_1"
AXES = (XA, YA, ZA, CA)
MESH_ID = pl.DeviceIdType.MESH
F32, BF16 = jnp.float32, jnp.bfloat16
TOK = 128


def far_first(n):
    return sorted(range(1, n), key=lambda d: (-min(d, n - d), d))


def nn(a, b):
    return lax.dot_general(a, b, (((1,), (0,)), ((), ())), preferred_element_type=F32)


def nt(a, b):
    return lax.dot_general(a, b, (((1,), (1,)), ((), ())), preferred_element_type=F32)


def row_sums(values):
    ones = jnp.ones((8, values.shape[1]), BF16)
    return nt(ones, values.astype(BF16))


def as_columns(row, width):
    col = jnp.broadcast_to(row[0:1, :], (TOK, TOK)).T
    return jnp.concatenate([col] * (width // TOK), axis=1)


class Links:
    def __init__(self, sizes, coords, send_sems, recv_sems):
        self.sizes, self.coords = sizes, coords
        self.ss, self.rs = send_sems, recv_sems
        self.used, self.sent = 0, []

    def fresh(self):
        k = self.used
        self.used += 1
        return k

    def copy(self, src, dst, device):
        k = self.fresh()
        return pltpu.make_async_remote_copy(
            src_ref=src,
            dst_ref=dst,
            send_sem=self.ss.at[k],
            recv_sem=self.rs.at[k],
            device_id=device,
            device_id_type=MESH_ID,
        )

    def start(self, src, dst, device):
        copy = self.copy(src, dst, device)
        copy.start()
        self.sent.append(copy)
        return copy

    def peer(self, axis, d):
        return lax.rem(self.coords[axis] + d, self.sizes[axis])

    def share(self, axis, ref, dst=None):
        dst = ref if dst is None else dst
        return {
            d: self.start(ref, dst, {axis: self.peer(axis, d)})
            for d in far_first(self.sizes[axis])
        }

    def local(self, src, dst):
        k = self.fresh()
        copy = pltpu.make_async_copy(src, dst, self.ss.at[k])
        copy.start()
        return copy


def arrived(copies):
    for copy in copies.values() if isinstance(copies, dict) else copies:
        copy.wait_recv()


def layer_kernel(
    sizes,
    x_in,
    og_in,
    wq_in,
    wk_in,
    wv_in,
    wo_in,
    wg_in,
    wu_in,
    wd_in,
    norm_a,
    norm_f,
    par_in,
    len_in,
    bias_in,
    out_ref,
    ig_ref,
    grad_ref,
    wqkv,
    wo,
    wgu,
    wd,
    gx,
    gog,
    gn,
    sq,
    bias_all,
    par_all,
    len_all,
    sb_qkv,
    rb_qkv,
    kv_pre,
    qkv_low,
    probs,
    gctx,
    sb_z,
    rb_z,
    fs_r,
    gfs,
    sb_gu,
    rb_gu,
    sb_dh,
    rb_dh,
    gdgu,
    ghid,
    gdot,
    pz,
    rb_dot,
    df_r,
    gdf,
    sb_dc,
    rb_dc,
    gdqkv,
    gv,
    tout,
    send_sems,
    recv_sems,
):
    nx, ny, nz, nc = sizes
    x, y, z, c = (lax.axis_index(a) for a in AXES)
    seqs = ny // nc
    s_h, hh_h = y // nc, y % nc
    a_r, s_r = z // seqs, z % seqs
    head_cols = wq_in.shape[1]
    ff_cols = wg_in.shape[1]
    rows = wq_in.shape[0]
    width = rows * nx * ny
    links = Links(dict(zip(AXES, sizes)), dict(zip(AXES, (x, y, z, c))), send_sems, recv_sems)

    partner = (x, nc * s_r + c, seqs * a_r + s_h, hh_h)
    at_home = jnp.logical_and(s_h == s_r, hh_h == c)
    away = jnp.logical_not(at_home)

    barrier = pltpu.get_barrier_semaphore()
    greeted = 0
    for axis, n in zip(AXES, sizes):
        for d in range(1, n):
            pl.semaphore_signal(
                barrier, inc=1, device_id={axis: links.peer(axis, d)}, device_id_type=MESH_ID
            )
            greeted += 1

    @pl.when(away)
    def _():
        pl.semaphore_signal(barrier, inc=1, device_id=partner, device_id_type=MESH_ID)
        pl.semaphore_wait(barrier, greeted + 1)

    @pl.when(at_home)
    def _():
        pl.semaphore_wait(barrier, greeted)

    def swapped(src, dst):
        away_copy = links.copy(src, dst, partner)
        k = links.fresh()
        home_copy = pltpu.make_async_copy(src, dst, links.ss.at[k])

        @pl.when(away)
        def _():
            away_copy.start()

        @pl.when(at_home)
        def _():
            home_copy.start()

        def done():
            @pl.when(away)
            def _():
                away_copy.wait()

            @pl.when(at_home)
            def _():
                home_copy.wait()

        return done

    z_there = seqs * a_r + s_h
    own_block = nc * z + c
    x_moved = swapped(x_in, gx.at[z_there])
    og_moved = swapped(
        og_in.at[:, pl.ds(pl.multiple_of(own_block * rows, rows), rows)], gog.at[z_there]
    )

    def w_spot(buf, col, n, there):
        spot = pl.ds(pl.multiple_of(there * rows, rows), rows)
        return buf.at[c, spot, pl.ds(col, n)]

    matrices = (
        ("q", wq_in, wqkv, 0),
        ("k", wk_in, wqkv, head_cols),
        ("v", wv_in, wqkv, 2 * head_cols),
        ("o", wo_in, wo, 0),
        ("d", wd_in, wd, 0),
        ("g", wg_in, wgu, 0),
        ("u", wu_in, wgu, ff_cols),
    )
    over_x, own_w, to_core = {}, {}, {}
    for name, src, buf, col in matrices:
        n = src.shape[1]
        over_x[name] = {
            d: links.start(src, w_spot(buf, col, n, x), {XA: links.peer(XA, d)})
            for d in far_first(nx)
        }
        own_w[name] = links.local(src, w_spot(buf, col, n, x))
        to_core[name] = [
            links.start(src, w_spot(buf, col, n, x), {CA: links.peer(CA, d)}) for d in range(1, nc)
        ]

    def relay(names):
        for name, src, buf, col in matrices:
            if name in names:
                for d, copy in over_x[name].items():
                    copy.wait_recv()
                    there = lax.rem(x + nx - d, nx)
                    spot = w_spot(buf, col, src.shape[1], there)
                    for e in range(1, nc):
                        to_core[name].append(links.start(spot, spot, {CA: links.peer(CA, e)}))

    def weights_ready(names):
        for name in names:
            own_w[name].wait()
            arrived(to_core[name])

    bias_here = links.local(bias_in, bias_all.at[c])
    small = [
        links.start(bias_in, bias_all.at[c], {CA: links.peer(CA, d)}) for d in range(1, nc)
    ]
    small += [links.start(par_in, par_all.at[c], {CA: links.peer(CA, d)}) for d in range(1, nc)]
    small += list(links.share(YA, len_in, len_all.at[y]).values())
    par_all[c] = par_in[...]
    len_all[y] = len_in[...]

    x_moved()
    x_gathered = links.share(ZA, gx.at[z])
    og_moved()
    og_gathered = links.share(ZA, gog.at[z])

    def wide(blocks, s):
        return jnp.concatenate([blocks[seqs * a + s] for a in range(nx)], axis=1)

    def gain(norm, a):
        return norm[ny * a + y]

    def normed(blocks, norm, k):
        for s in range(seqs):
            total = None
            for a in range(nx):
                v = blocks[seqs * a + s].astype(F32)
                gn[seqs * a + s] = (v * gain(norm, a)).astype(BF16)
                part = row_sums(v * v)
                total = part if total is None else total + part
            sq[k, y, s] = total
        return links.share(YA, sq.at[k, y])

    def inverse(k, s):
        total = sq[k, 0, s]
        for there in range(1, ny):
            total = total + sq[k, there, s]
        return lax.rsqrt(total / width + EPSILON)

    def scatter_y(blocks, weights, sent, landed):
        copies = {}
        for d in far_first(ny) + [0]:
            there = links.peer(YA, d) if d else y
            part = nn(wide(blocks, there // nc), weights[there % nc])
            if d == 0:
                return part, copies
            sent[d - 1] = part.astype(BF16)
            copies[d] = links.start(sent.at[d - 1], landed.at[d - 1], {YA: there})

    def total_of(own, landed, n):
        for d in range(n - 1):
            own = own + landed[d].astype(F32)
        return own

    def scatter_z(k, held, weights, extra=None):
        copies = {}
        for d in far_first(nz) + [0]:
            there = links.peer(ZA, d) if d else z
            a, s = there // seqs, there % seqs
            spot = pl.ds(pl.multiple_of(a * rows, rows), rows)
            part = None
            for hh in range(nc):
                term = nt(held[nc * s + hh], weights[hh, spot, :])
                part = term if part is None else part + term
            if d == 0:
                return part, copies
            sb_z[k, d - 1] = part.astype(BF16)
            copies[d] = links.start(sb_z.at[k, d - 1], rb_z.at[k, d - 1], {ZA: there})
            if extra is not None:
                copies[-d] = links.start(pz.at[extra, s], rb_dot.at[extra, d - 1], {ZA: there})

    def chip_sums(k):
        for s in range(seqs):
            total = gdot[k, nc * s]
            for hh in range(1, nc):
                total = total + gdot[k, nc * s + hh]
            pz[k, s] = total

    relay("qkv")
    arrived(x_gathered)
    sq1 = normed(gx, norm_a, 0)
    weights_ready("qkv")
    own, moved = scatter_y(gn, wqkv, sb_qkv, rb_qkv)
    bias_here.wait()
    arrived(small)
    relay("o")
    arrived(sq1)
    arrived(moved)
    inv_first = as_columns(inverse(0, s_h), 3 * head_cols)
    raw = total_of(own, rb_qkv, ny) * inv_first
    par = par_all[hh_h]
    scale_key = par[0:1, 0:head_cols]
    scale_value = par[0:1, head_cols : 2 * head_cols]
    scale_ffn = par[0:1, 2 * head_cols : 2 * head_cols + ff_cols]
    key_pre = raw[:, head_cols : 2 * head_cols]
    value_pre = raw[:, 2 * head_cols :]
    kv_pre[0] = key_pre
    kv_pre[1] = value_pre
    qkv_low[0] = raw[:, :head_cols].astype(BF16)
    qkv_low[1] = (key_pre * scale_key).astype(BF16)
    qkv_low[2] = (value_pre * scale_value).astype(BF16)
    lane = lax.broadcasted_iota(jnp.int32, (TOK, TOK), 1)
    real = lane.astype(F32) < len_all[nc * s_h + c][0:1, :]
    halves = [lane < HEAD_DIM, lane >= HEAD_DIM]
    zero = jnp.zeros((TOK, TOK), F32)

    def half_of(pair, half):
        return jnp.where(halves[half], pair.astype(F32), zero).astype(BF16)

    pairs = head_cols // TOK
    for pair in range(pairs):
        cols = slice(pair * TOK, (pair + 1) * TOK)
        q2, k2, v2 = (qkv_low[i, :, cols] for i in range(3))
        parts = []
        for half in range(2):
            head = 2 * pair + half
            scores = nt(half_of(q2, half), k2) + bias_all[hh_h, head]
            scores = jnp.where(real, scores, NEGATIVE)
            exponent = jnp.exp(scores - jnp.max(scores, axis=1, keepdims=True))
            prob = exponent / jnp.sum(exponent, axis=1, keepdims=True)
            probs[head] = prob
            parts.append(nn(prob.astype(BF16), v2))
        gctx[y, :, cols] = jnp.where(halves[0], parts[0], parts[1]).astype(BF16)
    ctx_gathered = links.share(YA, gctx.at[y])
    weights_ready("o")
    relay("d")
    arrived(ctx_gathered)
    own, moved = scatter_z(0, gctx, wo)
    weights_ready("d")
    arrived(og_gathered)
    own_dh, dh_moved = scatter_y(gog, wd, sb_dh, rb_dh)
    arrived(moved)
    first_sum = gx[z].astype(F32) + total_of(own, rb_z.at[0], nz)
    fs_r[...] = first_sum
    gfs[z] = first_sum.astype(BF16)
    fs_gathered = links.share(ZA, gfs.at[z])

    relay("gu")
    arrived(fs_gathered)
    sq2 = normed(gfs, norm_f, 1)
    weights_ready("gu")
    own, moved = scatter_y(gn, wgu, sb_gu, rb_gu)
    arrived(sq2)
    arrived(dh_moved)
    arrived(moved)
    d_hidden = total_of(own_dh, rb_dh, ny)
    both = total_of(own, rb_gu, ny) * as_columns(inverse(1, s_h), 2 * ff_cols)
    gate, up = both[:, :ff_cols], both[:, ff_cols:]
    root = math.sqrt(2.0 / math.pi)
    squared = gate * gate
    tanh = jnp.tanh(root * (gate + 0.044715 * gate * squared))
    activated = 0.5 * gate * (1.0 + tanh)
    slope = 0.5 * (1.0 + tanh) + 0.5 * gate * (1.0 - tanh * tanh) * (
        root * (1.0 + (3.0 * 0.044715) * squared)
    )
    product = activated * up
    d_product = d_hidden * scale_ffn
    d_gate = (d_product * up * slope).astype(BF16)
    d_up = (d_product * activated).astype(BF16)
    gdgu[y, :, :ff_cols] = d_gate
    gdgu[y, :, ff_cols:] = d_up
    dgu_gathered = links.share(YA, gdgu.at[y])
    gdot[0, y] = row_sums(d_gate.astype(F32) * gate + d_up.astype(F32) * up)
    dot_gathered = links.share(YA, gdot.at[0, y])
    ghid[y] = (product * scale_ffn).astype(BF16)
    hid_gathered = links.share(YA, ghid.at[y])
    grads_at = 2 * head_cols
    gv[0, 0, 0:1, grads_at:] = jnp.sum(d_hidden * product, axis=0, keepdims=True)
    arrived(dot_gathered)
    chip_sums(0)
    arrived(dgu_gathered)
    own, moved = scatter_z(1, gdgu, wgu, 0)
    inv_second = as_columns(inverse(1, s_r), rows)
    arrived(moved)
    dot = total_of(pz[0, s_r], rb_dot.at[0], nz)
    out_grad_r = gog[z].astype(F32)
    scaled = total_of(own, rb_z.at[1], nz) * gain(norm_f, a_r)
    d_first = (
        out_grad_r
        + inv_second * scaled
        - fs_r[...] * (inv_second * inv_second * as_columns(dot / width, rows))
    )
    df_r[...] = d_first
    gdf[z] = d_first.astype(BF16)
    df_gathered = links.share(ZA, gdf.at[z])
    arrived(hid_gathered)
    own_ff, ff_moved = scatter_z(2, ghid, wd)

    arrived(df_gathered)
    own, moved = scatter_y(gdf, wo, sb_dc, rb_dc)
    arrived(moved)
    d_context = total_of(own, rb_dc, ny).astype(BF16)
    for pair in range(pairs):
        cols = slice(pair * TOK, (pair + 1) * TOK)
        q2, k2, v2 = (qkv_low[i, :, cols] for i in range(3))
        dc2 = d_context[:, cols]
        dq, dk, dv = [], [], []
        for half in range(2):
            prob = probs[2 * pair + half]
            d_probs = nt(half_of(dc2, half), v2)
            inner = jnp.sum(prob * d_probs, axis=1, keepdims=True)
            d_scores = prob * (d_probs - inner)
            dq.append(nn(d_scores.astype(BF16), k2))
            dk.append(nn(d_scores.T.astype(BF16), q2))
            dv.append(nn(prob.T.astype(BF16), dc2))
        d_query, d_key, d_value = (jnp.where(halves[0], *two) for two in (dq, dk, dv))
        key2, value2 = kv_pre[0, :, cols], kv_pre[1, :, cols]
        at = pair * TOK
        gv[0, 0, 0:1, at : at + TOK] = jnp.sum(d_key * key2, axis=0, keepdims=True)
        at += head_cols
        gv[0, 0, 0:1, at : at + TOK] = jnp.sum(d_value * value2, axis=0, keepdims=True)
        d_query = d_query.astype(BF16)
        d_key = (d_key * scale_key[:, cols]).astype(BF16)
        d_value = (d_value * scale_value[:, cols]).astype(BF16)
        terms = (
            d_query.astype(F32) * q2.astype(F32)
            + d_key.astype(F32) * key2
            + d_value.astype(F32) * value2
        )
        sums = row_sums(terms)
        dots = sums if pair == 0 else dots + sums
        for i, part in enumerate((d_query, d_key, d_value)):
            gdqkv[y, :, i * head_cols + pair * TOK : i * head_cols + (pair + 1) * TOK] = part
    dqkv_gathered = links.share(YA, gdqkv.at[y])
    gdot[1, y] = dots
    dot_gathered = links.share(YA, gdot.at[1, y])

    gv_c = links.share(CA, gv.at[0, 0], gv.at[0, 1])
    arrived(ff_moved)
    tout[0] = (fs_r[...] + total_of(own_ff, rb_z.at[2], nz)).astype(BF16)
    out_moved = swapped(tout.at[0], tout.at[2])
    arrived(gv_c)
    total = gv[0, 0]
    if nc > 1:
        total = total + gv[0, 1]
    gv[1, y] = total
    gv_y = links.share(YA, gv.at[1, y])
    arrived(dot_gathered)
    chip_sums(1)
    arrived(dqkv_gathered)
    own, moved = scatter_z(3, gdqkv, wqkv, 1)
    arrived(gv_y)
    total = gv[1, c]
    for s in range(1, seqs):
        total = total + gv[1, nc * s + c]
    gv[2, x] = total
    gv_x = links.share(XA, gv.at[2, x])
    inv_first = as_columns(inverse(0, s_r), rows)
    arrived(moved)
    dot = total_of(pz[1, s_r], rb_dot.at[1], nz)
    scaled = total_of(own, rb_z.at[3], nz) * gain(norm_a, a_r)
    tout[1] = (
        df_r[...]
        + inv_first * scaled
        - gx[z].astype(F32) * (inv_first * inv_first * as_columns(dot / width, rows))
    ).astype(BF16)
    ig_moved = swapped(tout.at[1], tout.at[3])
    arrived(gv_x)
    total = gv[2, 0]
    for there in range(1, nx):
        total = total + gv[2, there]
    grad_ref[...] = total
    out_moved()
    out_ref[...] = tout[2]
    ig_moved()
    ig_ref[...] = tout[3]
    for copy in links.sent:
        copy.wait_send()


def on_device(
    sizes,
    hidden_in,
    lengths,
    norm_attn,
    q_weight,
    k_weight,
    v_weight,
    out_weight_t,
    norm_ffn,
    gate_weight,
    up_weight,
    down_weight_t,
    scale_key,
    scale_value,
    scale_ffn,
    out_grad,
    position_bias,
):
    nx, ny, nz, nc = sizes
    seqs = ny // nc
    rows, head_cols = q_weight.shape
    ff_cols = gate_weight.shape[1]
    blocks = nx * ny
    extra = 2 * head_cols + ff_cols
    par = jnp.broadcast_to(jnp.concatenate([scale_key, scale_value, scale_ffn])[None], (8, extra))
    lens = jnp.broadcast_to(lengths.astype(F32)[:, None], (8, TOK))
    heads = head_cols // HEAD_DIM
    wide = rows * nx
    vmem, hbm = pl.BlockSpec(memory_space=pltpu.VMEM), pl.BlockSpec(memory_space=pl.ANY)

    def buf(*shape, dtype=BF16):
        return pltpu.VMEM(shape, dtype)

    scratch = [
        buf(nc, wide, 3 * head_cols),
        buf(nc, wide, head_cols),
        buf(nc, wide, 2 * ff_cols),
        buf(nc, wide, ff_cols),
        buf(nz, TOK, rows),
        buf(nz, TOK, rows),
        buf(nz, TOK, rows),
        buf(2, ny, seqs, 8, TOK, dtype=F32),
        buf(nc, heads, TOK, TOK, dtype=F32),
        buf(nc, 8, extra, dtype=F32),
        buf(ny, 8, TOK, dtype=F32),
        buf(ny - 1, TOK, 3 * head_cols),
        buf(ny - 1, TOK, 3 * head_cols),
        buf(2, TOK, head_cols, dtype=F32),
        buf(3, TOK, head_cols),
        buf(heads, TOK, TOK, dtype=F32),
        buf(ny, TOK, head_cols),
        buf(4, nz - 1, TOK, rows),
        buf(4, nz - 1, TOK, rows),
        buf(TOK, rows, dtype=F32),
        buf(nz, TOK, rows),
        buf(ny - 1, TOK, 2 * ff_cols),
        buf(ny - 1, TOK, 2 * ff_cols),
        buf(ny - 1, TOK, ff_cols),
        buf(ny - 1, TOK, ff_cols),
        buf(ny, TOK, 2 * ff_cols),
        buf(ny, TOK, ff_cols),
        buf(2, ny, 8, TOK, dtype=F32),
        buf(2, seqs, 8, TOK, dtype=F32),
        buf(2, nz - 1, 8, TOK, dtype=F32),
        buf(TOK, rows, dtype=F32),
        buf(nz, TOK, rows),
        buf(ny - 1, TOK, head_cols),
        buf(ny - 1, TOK, head_cols),
        buf(ny, TOK, 3 * head_cols),
        buf(3, max(nx, ny, 2), 8, extra, dtype=F32),
        buf(4, TOK, rows),
        pltpu.SemaphoreType.DMA((256,)),
        pltpu.SemaphoreType.DMA((256,)),
    ]
    block_out, input_grad, grads = pl.pallas_call(
        functools.partial(layer_kernel, sizes),
        out_shape=(
            jax.ShapeDtypeStruct((TOK, rows), BF16),
            jax.ShapeDtypeStruct((TOK, rows), BF16),
            jax.ShapeDtypeStruct((8, extra), F32),
        ),
        in_specs=[hbm] * 9 + [vmem] * 4 + [hbm],
        out_specs=(vmem,) * 3,
        scratch_shapes=scratch,
        compiler_params=pltpu.CompilerParams(
            collective_id=0, has_side_effects=True, vmem_limit_bytes=60 * 1024 * 1024
        ),
    )(
        hidden_in,
        out_grad,
        q_weight,
        k_weight,
        v_weight,
        out_weight_t,
        gate_weight,
        up_weight,
        down_weight_t,
        norm_attn.reshape(blocks, 1, rows),
        norm_ffn.reshape(blocks, 1, rows),
        par,
        lens,
        position_bias,
    )
    grads = grads[0]
    return (
        block_out,
        input_grad,
        grads[:head_cols],
        grads[head_cols : 2 * head_cols],
        grads[2 * head_cols :],
    )


def solution(mesh, sizes=(4, 4, 8, 2)):
    finer = Mesh(mesh.devices.reshape(sizes), AXES)
    dp, mp = (XA, YA), (ZA, CA)
    placed = (
        P(dp, mp),
        P(dp),
        P(),
        P(dp, mp),
        P(dp, mp),
        P(dp, mp),
        P(dp, mp),
        P(),
        P(dp, mp),
        P(dp, mp),
        P(dp, mp),
        P(mp),
        P(mp),
        P(mp),
        P(dp, None),
        P(mp, None, None),
    )
    return jax.shard_map(
        functools.partial(on_device, sizes),
        mesh=finer,
        in_specs=placed,
        out_specs=(P(dp, mp), P(dp, mp), P(mp), P(mp), P(mp)),
        check_vma=False,
    )
```

time: 440 us -> 194 us (0.44)
  waiting for transfers between devices: 211 us -> 0 us
  Pallas kernels: 0 us -> 186 us
  blocking collectives: 102 us -> 0 us
  matrix products: 49.2 us -> 0 us
  starting transfers between devices: 24.1 us -> 0 us
  other arithmetic: 17.2 us -> 0.72 us
  between operations: 15.3 us -> 1.3 us
  local copies, waits for them, and re-layouts: 17.2 us -> 5.97 us
    all_gather x2 -> x0, waiting for transfers between devices: 187 us -> none  [the longest x1 153 us: side_by_side(): lax.all_gather(both, axis, axis=dim, tiled=True)]
    pallas_call x0 -> x1, Pallas kernels: none -> 186 us  [on_device(): pl.pallas_call(functools.partial(layer_kernel, sizes), out_shape=(jax.Sha...]
    all_to_all x7 -> x0, blocking collectives: 84.8 us -> none  [the longest x2 41.6 us: summed_rows(): lax.all_to_all(nearer.astype(jnp.bfloat16), far, split_axis=0, concat_axi...]
    dot_general x20 -> x0, matrix products: 49.2 us -> none  [the longest x7 22.8 us: contract_last(): lax.dot_general(left_side, right_side, (((1,), (1,)), ((), ())), preferre...]
    all_to_all x4 -> x0, starting transfers between devices: 24 us -> none  [the longest x2 13.2 us: from_everyone(): return lax.all_to_all(copies, axis, split_axis=0, concat_axis=0, tiled=True)]
    all_to_all x4 -> x0, waiting for transfers between devices: 22.9 us -> none  [the longest x2 15.6 us: from_everyone(): return lax.all_to_all(copies, axis, split_axis=0, concat_axis=0, tiled=True)]
    psum x2 -> x0, blocking collectives: 17.4 us -> none  [over_axes(): return functools.reduce(lax.psum, axes, x)]
    reduce_sum x12 -> x0, other arithmetic: 11.5 us -> none  [the longest x4 5.53 us: summed_on_arrival(): return arrived.astype(jnp.float32).sum(axis=0)]
  transfers between devices with their start and end apart: 6 -> 0, of which waited for: 6 -> 0; matrix products, arithmetic and copies ran while one was open for 9% -> 0% of each run, Pallas kernels for 0% -> 0%
where the time goes in v1:
time: 194 us
  Pallas kernels  186 us (96%)
  local copies, waits for them, and re-layouts  5.97 us (3%)
    pallas_call x1, Pallas kernels, on_device(): pl.pallas_call(functools.partial(layer_kernel, sizes), out_shape=(jax.Sha...  186 us

profile of v1, /device:TPU:33, one launch (start us, length us, event | category | flops | bytes accessed | tf_op | source)
XLA Modules:
  0.0 193.9 jit_solution(7168337431112198932)
XLA Ops:
  0.6 0.7 pad_maximum_fusion
  1.4 0.6 broadcast_in_dim.6.par_in
  2.6 0.6 broadcast_in_dim.16.len_in
  3.2 185.9 %shard_map.191 = (bf16[128,256]{1,0:T(8,128)(2,1)}, bf16[128,256]{1,0:T(8,128)(2,1)}, f32[8,1152]{1,0:T(8,128)}) custom-call(bf16[128,256]{1,0:T(8,128)(2,1)} %x_in.1, bf16[128,4096]{1,0:T(8,128)(2,1)} %og_in.1, bf16[256,256]{1,0:T(8,128)(2,1)} %wq_in.1, bf16[256,256]{1,0:T(8,128)(2,1)} %wk_in.1, bf16[256,256]{1,0:T(8,128)(2,1)} %wv_in.1, ...), custom_call_target="tpu_custom_call" | custom-call | tf_op jit(solution)/shard_map/pallas_call | solution.py:600
  189.1 1.3 fusion
  190.4 1.3 slice_reduce_fusion
  191.8 0.0 copy-start
  191.8 1.5 copy.24
  193.3 0.0 copy-done
  193.3 0.6 copy.25
Async XLA Ops:
  191.8 1.5 copy-start

commit v2 on v1

v2 whole, which is shorter than its diff:
```python
import functools
import math

import jax
import jax.numpy as jnp
from jax import lax
from jax.experimental import pallas as pl
from jax.experimental.pallas import tpu as pltpu
from jax.sharding import Mesh
from jax.sharding import PartitionSpec as P

HEAD_DIM = 64
EPSILON = 1e-06
NEGATIVE = -1e30
XA, YA, ZA, CA = "dp_0", "dp_1", "mp_0", "mp_1"
AXES = (XA, YA, ZA, CA)
MESH_ID = pl.DeviceIdType.MESH
F32, BF16 = jnp.float32, jnp.bfloat16
TOK = 128
CUT = 2
PART = TOK // CUT


def far_first(n):
    return sorted(range(1, n), key=lambda d: (-min(d, n - d), d))


def nn(a, b):
    return lax.dot_general(a, b, (((1,), (0,)), ((), ())), preferred_element_type=F32)


def nt(a, b):
    return lax.dot_general(a, b, (((1,), (1,)), ((), ())), preferred_element_type=F32)


def row_sums(values):
    tokens, depth = values.shape
    if tokens < TOK:
        values = jnp.concatenate([values, jnp.zeros((TOK - tokens, depth), values.dtype)], axis=0)
    return nt(jnp.ones((8, depth), BF16), values.astype(BF16))


def as_columns(row):
    return jnp.broadcast_to(row[0:1, :], (TOK, TOK)).T


def widened(col, width):
    return jnp.concatenate([col] * (width // TOK), axis=1)


class Links:
    def __init__(self, sizes, coords, send_sems, recv_sems):
        self.sizes, self.coords = sizes, coords
        self.ss, self.rs = send_sems, recv_sems
        self.used, self.sent = 0, []

    def fresh(self):
        k = self.used
        self.used += 1
        return k

    def copy(self, src, dst, device):
        k = self.fresh()
        return pltpu.make_async_remote_copy(
            src_ref=src,
            dst_ref=dst,
            send_sem=self.ss.at[k],
            recv_sem=self.rs.at[k],
            device_id=device,
            device_id_type=MESH_ID,
        )

    def start(self, src, dst, device):
        copy = self.copy(src, dst, device)
        copy.start()
        self.sent.append(copy)
        return copy

    def peer(self, axis, d):
        return lax.rem(self.coords[axis] + d, self.sizes[axis])

    def share(self, axis, ref, dst=None):
        dst = ref if dst is None else dst
        return [
            self.start(ref, dst, {axis: self.peer(axis, d)}) for d in far_first(self.sizes[axis])
        ]

    def local(self, src, dst):
        k = self.fresh()
        copy = pltpu.make_async_copy(src, dst, self.ss.at[k])
        copy.start()
        return copy


def arrived(copies):
    for copy in copies:
        copy.wait_recv()


def layer_kernel(
    sizes,
    x_in,
    og_in,
    wq_in,
    wk_in,
    wv_in,
    wo_in,
    wg_in,
    wu_in,
    wd_in,
    bias_in,
    norm_a,
    norm_f,
    sk_in,
    sv_in,
    sf_in,
    len_in,
    out_ref,
    ig_ref,
    gk_ref,
    gv_ref,
    gf_ref,
    wqkv,
    wo,
    wgu,
    wd,
    gx,
    gog,
    gn,
    sq,
    inv,
    bias_all,
    par_all,
    len_all,
    sb_qkv,
    rb_qkv,
    kv_pre,
    qkv_low,
    probs,
    gctx,
    sb_z,
    rb_z,
    fs_r,
    gfs,
    sb_gu,
    rb_gu,
    sb_dh,
    rb_dh,
    gdgu,
    ghid,
    gdot,
    pz,
    rb_dot,
    df_r,
    gdf,
    sb_dc,
    rb_dc,
    gdqkv,
    gv,
    tout,
    send_sems,
    recv_sems,
):
    nx, ny, nz, nc = sizes
    x, y, z, c = (lax.axis_index(a) for a in AXES)
    seqs = ny // nc
    s_h, hh_h = y // nc, y % nc
    a_r, s_r = z // seqs, z % seqs
    head_cols = wq_in.shape[1]
    ff_cols = wg_in.shape[1]
    rows = wq_in.shape[0]
    width = rows * nx * ny
    links = Links(dict(zip(AXES, sizes)), dict(zip(AXES, (x, y, z, c))), send_sems, recv_sems)

    partner = (x, nc * s_r + c, seqs * a_r + s_h, hh_h)
    at_home = jnp.logical_and(s_h == s_r, hh_h == c)
    away = jnp.logical_not(at_home)

    barrier = pltpu.get_barrier_semaphore()
    greeted = 0
    for axis, n in zip(AXES, sizes):
        for d in range(1, n):
            pl.semaphore_signal(
                barrier, inc=1, device_id={axis: links.peer(axis, d)}, device_id_type=MESH_ID
            )
            greeted += 1

    @pl.when(away)
    def _():
        pl.semaphore_signal(barrier, inc=1, device_id=partner, device_id_type=MESH_ID)
        pl.semaphore_wait(barrier, greeted + 1)

    @pl.when(at_home)
    def _():
        pl.semaphore_wait(barrier, greeted)

    def swapped(src, dst):
        away_copy = links.copy(src, dst, partner)
        k = links.fresh()
        home_copy = pltpu.make_async_copy(src, dst, links.ss.at[k])

        @pl.when(away)
        def _():
            away_copy.start()

        @pl.when(at_home)
        def _():
            home_copy.start()

        def done():
            @pl.when(away)
            def _():
                away_copy.wait()

            @pl.when(at_home)
            def _():
                home_copy.wait()

        return done

    z_there = seqs * a_r + s_h
    own_block = nc * z + c
    cuts = range(CUT)
    x_moved = [
        swapped(x_in.at[pl.ds(h * PART, PART), :], gx.at[h, z_there]) for h in cuts
    ]

    def w_spot(buf, col, n, there, half=None):
        start, size = there * rows, rows
        if half is not None:
            size = rows // 2
            start = start + half * size
        return buf.at[c, pl.ds(pl.multiple_of(start, size), size), pl.ds(col, n)]

    matrices = {
        "q": (wq_in, wqkv, 0),
        "k": (wk_in, wqkv, head_cols),
        "v": (wv_in, wqkv, 2 * head_cols),
        "o": (wo_in, wo, 0),
        "d": (wd_in, wd, 0),
        "g": (wg_in, wgu, 0),
        "u": (wu_in, wgu, ff_cols),
    }
    over_x, second, own_w, to_core = {}, {}, {}, {}

    def send_weights(names):
        for name in names:
            src, buf, col = matrices[name]
            spot = w_spot(buf, col, src.shape[1], x)
            steps = (1, nx - 1) if nx > 2 else range(1, nx)
            over_x[name] = {d: links.start(src, spot, {XA: links.peer(XA, d)}) for d in steps}
            own_w[name] = links.local(src, spot)
            to_core[name] = [
                links.start(src, spot, {CA: links.peer(CA, d)}) for d in range(1, nc)
            ]

    def to_other_core(name, spot):
        for e in range(1, nc):
            to_core[name].append(links.start(spot, spot, {CA: links.peer(CA, e)}))

    def relay(names):
        for name in names:
            src, buf, col = matrices[name]
            second[name] = []
            for d, copy in over_x[name].items():
                copy.wait_recv()
                there = lax.rem(x + nx - d, nx)
                if nx > 2:
                    half = 0 if d == 1 else 1
                    part = w_spot(buf, col, src.shape[1], there, half)
                    second[name].append(
                        (half, links.start(part, part, {XA: links.peer(XA, d)}))
                    )
                to_other_core(name, w_spot(buf, col, src.shape[1], there))

    def relay_far(names):
        for name in names:
            src, buf, col = matrices[name]
            for half, copy in second[name]:
                copy.wait_recv()
                to_other_core(name, w_spot(buf, col, src.shape[1], lax.rem(x + 2, nx), half))

    def weights_ready(names):
        for name in names:
            own_w[name].wait()
            arrived(to_core[name])

    send_weights("qkv")
    len_all[y] = jnp.full((8, TOK), len_in[0], jnp.int32).astype(F32)
    og_moved = [
        swapped(
            og_in.at[
                pl.ds(h * PART, PART), pl.ds(pl.multiple_of(own_block * rows, rows), rows)
            ],
            gog.at[h, z_there],
        )
        for h in cuts
    ]
    bias_here = links.local(bias_in, bias_all.at[c])
    small = links.share(CA, bias_in, bias_all.at[c])
    at = 0
    for part in (sk_in, sv_in, sf_in):
        n = part.shape[1]
        small += links.share(CA, part, par_all.at[c, :, pl.ds(at, n)])
        par_all[c, :, at : at + n] = part[...]
        at += n
    small += links.share(YA, len_all.at[y])

    x_gathered = []
    for h in cuts:
        x_moved[h]()
        x_gathered.append(links.share(ZA, gx.at[h, z]))

    def stacked(blocks, a):
        return jnp.concatenate([blocks[seqs * a + s] for s in range(seqs)], axis=0)

    def wide(blocks):
        return jnp.concatenate([stacked(blocks, a) for a in range(nx)], axis=1)

    def gain(norm, a):
        return norm[ny * a + y]

    tall = seqs * PART

    def normed(k, h, blocks, norm):
        total = None
        for a in range(nx):
            v = stacked(blocks, a).astype(F32)
            gn[h, :, a * rows : (a + 1) * rows] = (v * gain(norm, a)).astype(BF16)
            part = row_sums(v * v)
            total = part if total is None else total + part
        sq[k, h, y] = total
        return links.share(YA, sq.at[k, h, y])

    def find_inverse(k, h):
        total = sq[k, h, 0]
        for there in range(1, ny):
            total = total + sq[k, h, there]
        inv[k, h] = as_columns(lax.rsqrt(total / width + EPSILON))

    def inverse(k, h, s, n):
        spot = pl.ds(pl.multiple_of(s * PART, PART), PART)
        return widened(inv[k, h, spot, :], n)

    def scatter_y(h, lhs, weights, sent, landed):
        copies = []
        for e in range(nc - 1, -1, -1):
            hh = (hh_h + e) % nc
            part = nn(lhs, weights[hh]).astype(BF16)
            for s in range(seqs):
                sent[h, e, s] = part[s * PART : (s + 1) * PART]
            for p in range(seqs - 1, -1, -1):
                slot = e * seqs + p
                if slot:
                    s = (s_h + p) % seqs
                    copies.append(
                        links.start(
                            sent.at[h, e, s], landed.at[h, slot - 1], {YA: nc * s + hh}
                        )
                    )
        return copies

    def total_y(h, sent, landed):
        total = sent[h, 0, s_h].astype(F32)
        for slot in range(ny - 1):
            total = total + landed[h, slot].astype(F32)
        return total

    def scatter_z(k, h, held, weights, extra=None):
        copies = []
        for e in sorted(range(nx), key=lambda e: (-min(e, nx - e), e)):
            a = (a_r + e) % nx
            spot = pl.ds(pl.multiple_of(a * rows, rows), rows)
            part = None
            for hh in range(nc):
                lhs = jnp.concatenate([held[h, nc * s + hh] for s in range(seqs)], axis=0)
                term = nt(lhs, weights[hh, spot, :])
                part = term if part is None else part + term
            part = part.astype(BF16)
            for s in range(seqs):
                sb_z[k, h, e, s] = part[s * PART : (s + 1) * PART]
            for p in range(seqs):
                slot = e * seqs + p
                if slot == 0:
                    continue
                s = (s_r + p) % seqs
                there = {ZA: seqs * a + s}
                copies.append(
                    links.start(sb_z.at[k, h, e, s], rb_z.at[k, h, slot - 1], there)
                )
                if extra is not None:
                    copies.append(
                        links.start(pz.at[extra, h, s], rb_dot.at[extra, h, slot - 1], there)
                    )
        return copies

    def total_z(k, h):
        total = sb_z[k, h, 0, s_r].astype(F32)
        for slot in range(nz - 1):
            total = total + rb_z[k, h, slot].astype(F32)
        return total

    def chip_sums(k, h):
        for s in range(seqs):
            total = gdot[k, h, nc * s]
            for hh in range(1, nc):
                total = total + gdot[k, h, nc * s + hh]
            pz[k, h, s] = total

    def mean_dot(k, h):
        total = pz[k, h, s_r]
        for slot in range(nz - 1):
            total = total + rb_dot[k, h, slot]
        return widened(as_columns(total / width)[:PART], rows)

    arrived(x_gathered[0])
    sq1 = [normed(0, 0, gx.at[0], norm_a)]
    relay("qkv")
    send_weights("odgu")
    for h in range(1, CUT):
        arrived(x_gathered[h])
        sq1.append(normed(0, h, gx.at[h], norm_a))
    relay_far("qkv")
    weights_ready("qkv")
    moved = [scatter_y(h, gn[h], wqkv, sb_qkv, rb_qkv) for h in cuts]
    og_gathered = []
    for h in cuts:
        og_moved[h]()
        og_gathered.append(links.share(ZA, gog.at[h, z]))
    bias_here.wait()
    arrived(small)
    relay("o")
    par = par_all[hh_h]
    scale_key = par[:, 0:head_cols]
    scale_value = par[:, head_cols : 2 * head_cols]
    scale_ffn = par[:, 2 * head_cols : 2 * head_cols + ff_cols]
    for h in cuts:
        arrived(sq1[h])
        find_inverse(0, h)
        arrived(moved[h])
        part = pl.ds(h * PART, PART)
        raw = total_y(h, sb_qkv, rb_qkv) * inverse(0, h, s_h, 3 * head_cols)
        key_pre = raw[:, head_cols : 2 * head_cols]
        value_pre = raw[:, 2 * head_cols :]
        kv_pre[0, part, :] = key_pre
        kv_pre[1, part, :] = value_pre
        qkv_low[0, part, :] = raw[:, :head_cols].astype(BF16)
        qkv_low[1, part, :] = (key_pre * scale_key).astype(BF16)
        qkv_low[2, part, :] = (value_pre * scale_value).astype(BF16)
    lane = lax.broadcasted_iota(jnp.int32, (TOK, TOK), 1)
    real = lane.astype(F32) < len_all[nc * s_h + c][0:1, :]
    halves = [lane < HEAD_DIM, lane >= HEAD_DIM]
    zero = jnp.zeros((TOK, TOK), F32)

    def half_of(pair, half):
        return jnp.where(halves[half], pair.astype(F32), zero).astype(BF16)

    pairs = head_cols // TOK
    for pair in range(pairs):
        cols = slice(pair * TOK, (pair + 1) * TOK)
        q2, k2, v2 = (qkv_low[i, :, cols] for i in range(3))
        parts = []
        for half in range(2):
            head = 2 * pair + half
            scores = nt(half_of(q2, half), k2) + bias_all[hh_h, head]
            scores = jnp.where(real, scores, NEGATIVE)
            exponent = jnp.exp(scores - jnp.max(scores, axis=1, keepdims=True))
            prob = exponent / jnp.sum(exponent, axis=1, keepdims=True)
            probs[head] = prob
            parts.append(nn(prob.astype(BF16), v2))
        context = jnp.where(halves[0], parts[0], parts[1]).astype(BF16)
        for h in cuts:
            gctx[h, y, :, cols] = context[h * PART : (h + 1) * PART]
    ctx_gathered = [links.share(YA, gctx.at[h, y]) for h in cuts]
    relay_far("o")
    relay("d")
    weights_ready("o")
    moved = []
    for h in cuts:
        arrived(ctx_gathered[h])
        moved.append(scatter_z(0, h, gctx, wo))
    fs_gathered = []
    for h in cuts:
        arrived(moved[h])
        first_sum = gx[h, z].astype(F32) + total_z(0, h)
        fs_r[h] = first_sum
        gfs[h, z] = first_sum.astype(BF16)
        fs_gathered.append(links.share(ZA, gfs.at[h, z]))
    relay("gu")
    relay_far("d")
    weights_ready("d")
    dh_moved = []
    for h in cuts:
        arrived(og_gathered[h])
        dh_moved.append(scatter_y(h, wide(gog.at[h]), wd, sb_dh, rb_dh))
    relay_far("gu")

    sq2, moved = [], []
    for h in cuts:
        arrived(fs_gathered[h])
        sq2.append(normed(1, h, gfs.at[h], norm_f))
        if h == 0:
            weights_ready("gu")
        moved.append(scatter_y(h, gn[h], wgu, sb_gu, rb_gu))
    root = math.sqrt(2.0 / math.pi)
    dgu_gathered, dot_gathered, hid_gathered = [], [], []
    for h in cuts:
        arrived(sq2[h])
        find_inverse(1, h)
        arrived(dh_moved[h])
        d_hidden = total_y(h, sb_dh, rb_dh)
        arrived(moved[h])
        both = total_y(h, sb_gu, rb_gu) * inverse(1, h, s_h, 2 * ff_cols)
        gate, up = both[:, :ff_cols], both[:, ff_cols:]
        squared = gate * gate
        tanh = jnp.tanh(root * (gate + 0.044715 * gate * squared))
        activated = 0.5 * gate * (1.0 + tanh)
        slope = 0.5 * (1.0 + tanh) + 0.5 * gate * (1.0 - tanh * tanh) * (
            root * (1.0 + (3.0 * 0.044715) * squared)
        )
        product = activated * up
        d_product = d_hidden * scale_ffn
        d_gate = (d_product * up * slope).astype(BF16)
        d_up = (d_product * activated).astype(BF16)
        gdgu[h, y, :, :ff_cols] = d_gate
        gdgu[h, y, :, ff_cols:] = d_up
        dgu_gathered.append(links.share(YA, gdgu.at[h, y]))
        gdot[0, h, y] = row_sums(d_gate.astype(F32) * gate + d_up.astype(F32) * up)
        dot_gathered.append(links.share(YA, gdot.at[0, h, y]))
        ghid[h, y] = (product * scale_ffn).astype(BF16)
        part = jnp.sum(d_hidden * product, axis=0, keepdims=True)
        sums = part if h == 0 else sums + part
    hid_gathered = [links.share(YA, ghid.at[h, y]) for h in cuts]
    gv[0, 0, :, 2 * head_cols :] = sums
    moved = []
    for h in cuts:
        arrived(dot_gathered[h])
        chip_sums(0, h)
        arrived(dgu_gathered[h])
        moved.append(scatter_z(1, h, gdgu, wgu, 0))
    df_gathered = []
    for h in cuts:
        inv_second = inverse(1, h, s_r, rows)
        arrived(moved[h])
        d_first = (
            gog[h, z].astype(F32)
            + inv_second * (total_z(1, h) * gain(norm_f, a_r))
            - fs_r[h] * (inv_second * inv_second * mean_dot(0, h))
        )
        df_r[h] = d_first
        gdf[h, z] = d_first.astype(BF16)
        df_gathered.append(links.share(ZA, gdf.at[h, z]))

    moved = []
    for h in cuts:
        arrived(df_gathered[h])
        moved.append(scatter_y(h, wide(gdf.at[h]), wo, sb_dc, rb_dc))
    ff_moved = []
    for h in cuts:
        arrived(hid_gathered[h])
        ff_moved.append(scatter_z(2, h, ghid, wd))
    d_context = []
    for h in cuts:
        arrived(moved[h])
        d_context.append(total_y(h, sb_dc, rb_dc).astype(BF16))
    d_context = jnp.concatenate(d_context, axis=0)
    for pair in range(pairs):
        cols = slice(pair * TOK, (pair + 1) * TOK)
        q2, k2, v2 = (qkv_low[i, :, cols] for i in range(3))
        dc2 = d_context[:, cols]
        dq, dk, dv = [], [], []
        for half in range(2):
            prob = probs[2 * pair + half]
            d_probs = nt(half_of(dc2, half), v2)
            inner = jnp.sum(prob * d_probs, axis=1, keepdims=True)
            d_scores = prob * (d_probs - inner)
            dq.append(nn(d_scores.astype(BF16), k2))
            dk.append(nn(d_scores.T.astype(BF16), q2))
            dv.append(nn(prob.T.astype(BF16), dc2))
        d_query, d_key, d_value = (jnp.where(halves[0], *two) for two in (dq, dk, dv))
        key2, value2 = kv_pre[0, :, cols], kv_pre[1, :, cols]
        at = pair * TOK
        gv[0, 0, :, at : at + TOK] = jnp.sum(d_key * key2, axis=0, keepdims=True)
        at += head_cols
        gv[0, 0, :, at : at + TOK] = jnp.sum(d_value * value2, axis=0, keepdims=True)
        d_query = d_query.astype(BF16)
        d_key = (d_key * scale_key[:, cols]).astype(BF16)
        d_value = (d_value * scale_value[:, cols]).astype(BF16)
        terms = (
            d_query.astype(F32) * q2.astype(F32)
            + d_key.astype(F32) * key2
            + d_value.astype(F32) * value2
        )
        sums = [row_sums(terms[h * PART : (h + 1) * PART]) for h in cuts]
        dots = sums if pair == 0 else [old + new for old, new in zip(dots, sums)]
        for i, part in enumerate((d_query, d_key, d_value)):
            at = i * head_cols + pair * TOK
            for h in cuts:
                gdqkv[h, y, :, at : at + TOK] = part[h * PART : (h + 1) * PART]
    dqkv_gathered, dot_gathered = [], []
    for h in cuts:
        gdot[1, h, y] = dots[h]
        dot_gathered.append(links.share(YA, gdot.at[1, h, y]))
        dqkv_gathered.append(links.share(YA, gdqkv.at[h, y]))

    gv_c = links.share(CA, gv.at[0, 0], gv.at[0, 1])
    out_moved = []
    for h in cuts:
        arrived(ff_moved[h])
        tout[0, h] = (fs_r[h] + total_z(2, h)).astype(BF16)
        out_moved.append(swapped(tout.at[0, h], tout.at[2, h]))
    arrived(gv_c)
    total = gv[0, 0]
    if nc > 1:
        total = total + gv[0, 1]
    gv[1, y] = total
    gv_y = links.share(YA, gv.at[1, y])
    moved = []
    for h in cuts:
        arrived(dot_gathered[h])
        chip_sums(1, h)
        arrived(dqkv_gathered[h])
        moved.append(scatter_z(3, h, gdqkv, wqkv, 1))
    arrived(gv_y)
    total = gv[1, c]
    for s in range(1, seqs):
        total = total + gv[1, nc * s + c]
    gv[2, x] = total
    gv_x = links.share(XA, gv.at[2, x])
    ig_moved = []
    for h in cuts:
        inv_first = inverse(0, h, s_r, rows)
        arrived(moved[h])
        tout[1, h] = (
            df_r[h]
            + inv_first * (total_z(3, h) * gain(norm_a, a_r))
            - gx[h, z].astype(F32) * (inv_first * inv_first * mean_dot(1, h))
        ).astype(BF16)
        ig_moved.append(swapped(tout.at[1, h], tout.at[3, h]))
    arrived(gv_x)
    total = gv[2, 0]
    for there in range(1, nx):
        total = total + gv[2, there]
    gk_ref[...] = total[:, :head_cols]
    gv_ref[...] = total[:, head_cols : 2 * head_cols]
    gf_ref[...] = total[:, 2 * head_cols :]
    for h in cuts:
        part = pl.ds(h * PART, PART)
        out_moved[h]()
        out_ref[part, :] = tout[2, h]
        ig_moved[h]()
        ig_ref[part, :] = tout[3, h]
    for copy in links.sent:
        copy.wait_send()


def on_device(
    sizes,
    hidden_in,
    lengths,
    norm_attn,
    q_weight,
    k_weight,
    v_weight,
    out_weight_t,
    norm_ffn,
    gate_weight,
    up_weight,
    down_weight_t,
    scale_key,
    scale_value,
    scale_ffn,
    out_grad,
    position_bias,
):
    nx, ny, nz, nc = sizes
    seqs = ny // nc
    rows, head_cols = q_weight.shape
    ff_cols = gate_weight.shape[1]
    blocks = nx * ny
    extra = 2 * head_cols + ff_cols
    heads = head_cols // HEAD_DIM
    wide = rows * nx
    vmem, hbm = pl.BlockSpec(memory_space=pltpu.VMEM), pl.BlockSpec(memory_space=pl.ANY)
    smem = pl.BlockSpec(memory_space=pltpu.SMEM)

    def buf(*shape, dtype=BF16):
        return pltpu.VMEM(shape, dtype)

    scratch = [
        buf(nc, wide, 3 * head_cols),
        buf(nc, wide, head_cols),
        buf(nc, wide, 2 * ff_cols),
        buf(nc, wide, ff_cols),
        buf(CUT, nz, PART, rows),
        buf(CUT, nz, PART, rows),
        buf(CUT, seqs * PART, wide),
        buf(2, CUT, ny, 8, TOK, dtype=F32),
        buf(2, CUT, TOK, TOK, dtype=F32),
        buf(nc, heads, TOK, TOK, dtype=F32),
        buf(nc, 1, extra, dtype=F32),
        buf(ny, 8, TOK, dtype=F32),
        buf(CUT, nc, seqs, PART, 3 * head_cols),
        buf(CUT, ny - 1, PART, 3 * head_cols),
        buf(2, TOK, head_cols, dtype=F32),
        buf(3, TOK, head_cols),
        buf(heads, TOK, TOK, dtype=F32),
        buf(CUT, ny, PART, head_cols),
        buf(4, CUT, nx, seqs, PART, rows),
        buf(4, CUT, nz - 1, PART, rows),
        buf(CUT, PART, rows, dtype=F32),
        buf(CUT, nz, PART, rows),
        buf(CUT, nc, seqs, PART, 2 * ff_cols),
        buf(CUT, ny - 1, PART, 2 * ff_cols),
        buf(CUT, nc, seqs, PART, ff_cols),
        buf(CUT, ny - 1, PART, ff_cols),
        buf(CUT, ny, PART, 2 * ff_cols),
        buf(CUT, ny, PART, ff_cols),
        buf(2, CUT, ny, 8, TOK, dtype=F32),
        buf(2, CUT, seqs, 8, TOK, dtype=F32),
        buf(2, CUT, nz - 1, 8, TOK, dtype=F32),
        buf(CUT, PART, rows, dtype=F32),
        buf(CUT, nz, PART, rows),
        buf(CUT, nc, seqs, PART, head_cols),
        buf(CUT, ny - 1, PART, head_cols),
        buf(CUT, ny, PART, 3 * head_cols),
        buf(3, max(nx, ny, 2), 1, extra, dtype=F32),
        buf(4, CUT, PART, rows),
        pltpu.SemaphoreType.DMA((448,)),
        pltpu.SemaphoreType.DMA((448,)),
    ]
    block_out, input_grad, grad_key, grad_value, grad_ffn = pl.pallas_call(
        functools.partial(layer_kernel, sizes),
        out_shape=(
            jax.ShapeDtypeStruct((TOK, rows), BF16),
            jax.ShapeDtypeStruct((TOK, rows), BF16),
            jax.ShapeDtypeStruct((1, head_cols), F32),
            jax.ShapeDtypeStruct((1, head_cols), F32),
            jax.ShapeDtypeStruct((1, ff_cols), F32),
        ),
        in_specs=[hbm] * 10 + [vmem] * 5 + [smem],
        out_specs=(vmem,) * 5,
        scratch_shapes=scratch,
        compiler_params=pltpu.CompilerParams(
            collective_id=0, has_side_effects=True, vmem_limit_bytes=60 * 1024 * 1024
        ),
    )(
        hidden_in,
        out_grad,
        q_weight,
        k_weight,
        v_weight,
        out_weight_t,
        gate_weight,
        up_weight,
        down_weight_t,
        position_bias,
        norm_attn.reshape(blocks, 1, rows),
        norm_ffn.reshape(blocks, 1, rows),
        scale_key[None],
        scale_value[None],
        scale_ffn[None],
        lengths,
    )
    return block_out, input_grad, grad_key[0], grad_value[0], grad_ffn[0]


def solution(mesh, sizes=(4, 4, 8, 2)):
    finer = Mesh(mesh.devices.reshape(sizes), AXES)
    dp, mp = (XA, YA), (ZA, CA)
    placed = (
        P(dp, mp),
        P(dp),
        P(),
        P(dp, mp),
        P(dp, mp),
        P(dp, mp),
        P(dp, mp),
        P(),
        P(dp, mp),
        P(dp, mp),
        P(dp, mp),
        P(mp),
        P(mp),
        P(mp),
        P(dp, None),
        P(mp, None, None),
    )
    return jax.shard_map(
        functools.partial(on_device, sizes),
        mesh=finer,
        in_specs=placed,
        out_specs=(P(dp, mp), P(dp, mp), P(mp), P(mp), P(mp)),
        check_vma=False,
    )
```

time: 194 us -> 186 us (0.959)
  Pallas kernels: 186 us -> 178 us
    pallas_call x1, Pallas kernels: 186 us -> 178 us  [on_device(): pl.pallas_call(functools.partial(layer_kernel, sizes), out_shape=(jax.Sha...]
    slice x2 -> x0, local copies, waits for them, and re-layouts: 2.61 us -> none  [the longest x1 1.33 us: on_device(): grads[2 * head_cols:]]
    unnamed x4 -> x12, local copies, waits for them, and re-layouts: 2.14 us -> 4.03 us
where the time goes in v2:
time: 186 us; the launch traced here: 185 us
  Pallas kernels  178 us (96%)
  local copies, waits for them, and re-layouts  5.29 us (3%)
    pallas_call x1, Pallas kernels, on_device(): pl.pallas_call(functools.partial(layer_kernel, sizes), out_shape=(jax.Sha...  178 us
    unnamed x12, local copies, waits for them, and re-layouts  4.03 us

profile of v2, /device:TPU:33, one launch (start us, length us, event | category | flops | bytes accessed | tf_op | source)
XLA Modules:
  0.0 185.5 jit_solution(11193508959304131807)
XLA Ops:
  0.6 1.3 broadcast_in_dim.11.sf_in
  2.5 178.2 %shard_map.191 = (bf16[128,256]{1,0:T(8,128)(2,1)}, bf16[128,256]{1,0:T(8,128)(2,1)}, f32[1,256]{1,0:T(1,128)}, f32[1,256]{1,0:T(1,128)}, f32[1,640]{1,0:T(1,128)}) custom-call(bf16[128,256]{1,0:T(8,128)(2,1)} %x_in.1, bf16[128,4096]{1,0:T(8,128)(2,1)} %og_in.1, bf16[256,256]{1,0:T(8,128)(2,1)} %wq_in.1, bf16[256,256]{1,0:T(8,128)(2,1)} %wk_in.1, ...), custom_call_target="tpu_custom_call" | custom-call | tf_op jit(solution)/shard_map/pallas_call | solution.py:732
  180.8 0.0 copy-start.1
  180.8 0.7 copy-done.1
  181.5 0.6 reduce
  182.1 0.0 copy-start
  182.1 1.5 copy.26
  183.6 0.0 copy-done
  183.6 0.0 copy-start.3
  183.6 0.6 copy.27
  184.2 0.0 copy-done.3
  184.3 0.0 copy-start.2
  184.3 0.6 copy.28
  184.8 0.1 copy-done.2
  184.9 0.6 copy.29
Async XLA Ops:
  180.8 0.7 copy-start.1
  182.1 1.5 copy-start
  183.6 0.7 copy-start.3
  184.3 0.6 copy-start.2

commit v3 on v2

--- a/solution.py
+++ b/solution.py
@@ -17,7 +17,7 @@
 MESH_ID = pl.DeviceIdType.MESH
 F32, BF16 = jnp.float32, jnp.bfloat16
 TOK = 128
-CUT = 2
+CUT = 4
 PART = TOK // CUT
 
 
@@ -285,7 +285,7 @@
             own_w[name].wait()
             arrived(to_core[name])
 
-    send_weights("qkv")
+    send_weights("qkvo")
     len_all[y] = jnp.full((8, TOK), len_in[0], jnp.int32).astype(F32)
     og_moved = [
         swapped(
@@ -310,6 +310,8 @@
     for h in cuts:
         x_moved[h]()
         x_gathered.append(links.share(ZA, gx.at[h, z]))
+    relay("qkvo")
+    send_weights("dgu")
 
     def stacked(blocks, a):
         return jnp.concatenate([blocks[seqs * a + s] for s in range(seqs)], axis=0)
@@ -415,8 +417,6 @@
 
     arrived(x_gathered[0])
     sq1 = [normed(0, 0, gx.at[0], norm_a)]
-    relay("qkv")
-    send_weights("odgu")
     for h in range(1, CUT):
         arrived(x_gathered[h])
         sq1.append(normed(0, h, gx.at[h], norm_a))
@@ -429,7 +429,9 @@
         og_gathered.append(links.share(ZA, gog.at[h, z]))
     bias_here.wait()
     arrived(small)
-    relay("o")
+    relay_far("o")
+    weights_ready("o")
+    relay("d")
     par = par_all[hh_h]
     scale_key = par[:, 0:head_cols]
     scale_value = par[:, head_cols : 2 * head_cols]
@@ -472,44 +474,47 @@
         for h in cuts:
             gctx[h, y, :, cols] = context[h * PART : (h + 1) * PART]
     ctx_gathered = [links.share(YA, gctx.at[h, y]) for h in cuts]
-    relay_far("o")
-    relay("d")
-    weights_ready("o")
-    moved = []
-    for h in cuts:
+
+    root = math.sqrt(2.0 / math.pi)
+    out_sums, first, second_norm, hidden_dots = {}, {}, {}, {}
+    partial, dgu_gathered, hid_gathered, d_out, df_gathered, dc_moved = {}, {}, {}, {}, {}, {}
+    dh_moved, sums = {}, []
+
+    def out_product(h):
         arrived(ctx_gathered[h])
-        moved.append(scatter_z(0, h, gctx, wo))
-    fs_gathered = []
-    for h in cuts:
-        arrived(moved[h])
+        out_sums[h] = scatter_z(0, h, gctx, wo)
+
+    def first_residual(h):
+        arrived(out_sums[h])
         first_sum = gx[h, z].astype(F32) + total_z(0, h)
         fs_r[h] = first_sum
         gfs[h, z] = first_sum.astype(BF16)
-        fs_gathered.append(links.share(ZA, gfs.at[h, z]))
-    relay("gu")
-    relay_far("d")
-    weights_ready("d")
-    dh_moved = []
-    for h in cuts:
-        arrived(og_gathered[h])
-        dh_moved.append(scatter_y(h, wide(gog.at[h]), wd, sb_dh, rb_dh))
-    relay_far("gu")
-
-    sq2, moved = [], []
-    for h in cuts:
-        arrived(fs_gathered[h])
-        sq2.append(normed(1, h, gfs.at[h], norm_f))
+        first[h] = links.share(ZA, gfs.at[h, z])
+
+    def hidden_grads():
+        relay("gu")
+        relay_far("d")
+        weights_ready("d")
+        for h in cuts:
+            arrived(og_gathered[h])
+            dh_moved[h] = scatter_y(h, wide(gog.at[h]), wd, sb_dh, rb_dh)
+        relay_far("gu")
+
+    def gate_and_up(h):
+        if h == 0:
+            hidden_grads()
+        arrived(first[h])
+        second_norm[h] = normed(1, h, gfs.at[h], norm_f)
         if h == 0:
             weights_ready("gu")
-        moved.append(scatter_y(h, gn[h], wgu, sb_gu, rb_gu))
-    root = math.sqrt(2.0 / math.pi)
-    dgu_gathered, dot_gathered, hid_gathered = [], [], []
-    for h in cuts:
-        arrived(sq2[h])
+        partial[h] = scatter_y(h, gn[h], wgu, sb_gu, rb_gu)
+
+    def hidden_units(h):
+        arrived(second_norm[h])
         find_inverse(1, h)
         arrived(dh_moved[h])
         d_hidden = total_y(h, sb_dh, rb_dh)
-        arrived(moved[h])
+        arrived(partial[h])
         both = total_y(h, sb_gu, rb_gu) * inverse(1, h, s_h, 2 * ff_cols)
         gate, up = both[:, :ff_cols], both[:, ff_cols:]
         squared = gate * gate
@@ -524,24 +529,28 @@
         d_up = (d_product * activated).astype(BF16)
         gdgu[h, y, :, :ff_cols] = d_gate
         gdgu[h, y, :, ff_cols:] = d_up
-        dgu_gathered.append(links.share(YA, gdgu.at[h, y]))
+        dgu_gathered[h] = links.share(YA, gdgu.at[h, y])
         gdot[0, h, y] = row_sums(d_gate.astype(F32) * gate + d_up.astype(F32) * up)
-        dot_gathered.append(links.share(YA, gdot.at[0, h, y]))
+        hidden_dots[h] = links.share(YA, gdot.at[0, h, y])
         ghid[h, y] = (product * scale_ffn).astype(BF16)
-        part = jnp.sum(d_hidden * product, axis=0, keepdims=True)
-        sums = part if h == 0 else sums + part
-    hid_gathered = [links.share(YA, ghid.at[h, y]) for h in cuts]
-    gv[0, 0, :, 2 * head_cols :] = sums
-    moved = []
-    for h in cuts:
-        arrived(dot_gathered[h])
+        sums.append(jnp.sum(d_hidden * product, axis=0, keepdims=True))
+        if h == CUT - 1:
+            for i in cuts:
+                hid_gathered[i] = links.share(YA, ghid.at[i, y])
+            total = sums[0]
+            for part in sums[1:]:
+                total = total + part
+            gv[0, 0, :, 2 * head_cols :] = total
+
+    def second_grad(h):
+        arrived(hidden_dots[h])
         chip_sums(0, h)
         arrived(dgu_gathered[h])
-        moved.append(scatter_z(1, h, gdgu, wgu, 0))
-    df_gathered = []
-    for h in cuts:
+        d_out[h] = scatter_z(1, h, gdgu, wgu, 0)
+
+    def first_grad(h):
         inv_second = inverse(1, h, s_r, rows)
-        arrived(moved[h])
+        arrived(d_out[h])
         d_first = (
             gog[h, z].astype(F32)
             + inv_second * (total_z(1, h) * gain(norm_f, a_r))
@@ -549,19 +558,32 @@
         )
         df_r[h] = d_first
         gdf[h, z] = d_first.astype(BF16)
-        df_gathered.append(links.share(ZA, gdf.at[h, z]))
-
-    moved = []
-    for h in cuts:
+        df_gathered[h] = links.share(ZA, gdf.at[h, z])
+
+    def context_grad(h):
         arrived(df_gathered[h])
-        moved.append(scatter_y(h, wide(gdf.at[h]), wo, sb_dc, rb_dc))
+        dc_moved[h] = scatter_y(h, wide(gdf.at[h]), wo, sb_dc, rb_dc)
+
+    wave = (
+        out_product,
+        first_residual,
+        gate_and_up,
+        hidden_units,
+        second_grad,
+        first_grad,
+        context_grad,
+    )
+    for step in range(len(wave) + CUT - 1):
+        for k, stage in enumerate(wave):
+            if 0 <= step - k < CUT:
+                stage(step - k)
     ff_moved = []
     for h in cuts:
         arrived(hid_gathered[h])
         ff_moved.append(scatter_z(2, h, ghid, wd))
     d_context = []
     for h in cuts:
-        arrived(moved[h])
+        arrived(dc_moved[h])
         d_context.append(total_y(h, sb_dc, rb_dc).astype(BF16))
     d_context = jnp.concatenate(d_context, axis=0)
     for pair in range(pairs):
@@ -652,6 +674,14 @@
         ig_ref[part, :] = tout[3, h]
     for copy in links.sent:
         copy.wait_send()
+
+
+def publish_kernel(out_in, ig_in, gk_in, gv_in, gf_in, out_ref, ig_ref, gk_ref, gv_ref, gf_ref):
+    out_ref[...] = out_in[...]
+    ig_ref[...] = ig_in[...]
+    gk_ref[...] = gk_in[...]
+    gv_ref[...] = gv_in[...]
+    gf_ref[...] = gf_in[0]
 
 
 def on_device(
@@ -726,8 +756,8 @@
         buf(CUT, ny, PART, 3 * head_cols),
         buf(3, max(nx, ny, 2), 1, extra, dtype=F32),
         buf(4, CUT, PART, rows),
-        pltpu.SemaphoreType.DMA((448,)),
-        pltpu.SemaphoreType.DMA((448,)),
+        pltpu.SemaphoreType.DMA((640,)),
+        pltpu.SemaphoreType.DMA((640,)),
     ]
     block_out, input_grad, grad_key, grad_value, grad_ffn = pl.pallas_call(
         functools.partial(layer_kernel, sizes),
@@ -762,7 +792,20 @@
         scale_ffn[None],
         lengths,
     )
-    return block_out, input_grad, grad_key[0], grad_value[0], grad_ffn[0]
+    results = pl.pallas_call(
+        publish_kernel,
+        out_shape=(
+            jax.ShapeDtypeStruct((TOK, rows), BF16),
+            jax.ShapeDtypeStruct((TOK, rows), BF16),
+            jax.ShapeDtypeStruct((1, head_cols), F32),
+            jax.ShapeDtypeStruct((1, head_cols), F32),
+            jax.ShapeDtypeStruct((ff_cols,), F32),
+        ),
+        in_specs=[vmem] * 5,
+        out_specs=(vmem,) * 5,
+    )(block_out, input_grad, grad_key, grad_value, grad_ffn)
+    block_out, input_grad, grad_key, grad_value, grad_ffn = results
+    return block_out, input_grad, grad_key[0], grad_value[0], grad_ffn
 
 
 def solution(mesh, sizes=(4, 4, 8, 2)):

time: 186 us -> 169 us (0.909)
  Pallas kernels: 178 us -> 166 us
  local copies, waits for them, and re-layouts: 5.29 us -> 1.26 us
    pallas_call x1, Pallas kernels: 178 us -> 164 us  [on_device(): pl.pallas_call(functools.partial(layer_kernel, sizes), out_shape=(jax.Sha...]
    unnamed x12 -> x2, local copies, waits for them, and re-layouts: 4.03 us -> 0.68 us
where the time goes in v3:
time: 169 us
  Pallas kernels  166 us (98%)
    pallas_call x1, Pallas kernels, on_device(): pl.pallas_call(functools.partial(layer_kernel, sizes), out_shape=(jax.Sha...  164 us

profile of v3, /device:TPU:33, one launch (start us, length us, event | category | flops | bytes accessed | tf_op | source)
XLA Modules:
  0.0 168.5 jit_solution(14019543379605284207)
XLA Ops:
  1.3 0.0 copy-start
  1.3 0.7 copy-done
  2.0 0.6 broadcast_in_dim.11.sf_in
  2.5 164.4 %shard_map.191 = (bf16[128,256]{1,0:T(8,128)(2,1)}, bf16[128,256]{1,0:T(8,128)(2,1)}, f32[1,256]{1,0:T(1,128)}, f32[1,256]{1,0:T(1,128)}, f32[1,640]{1,0:T(1,128)}) custom-call(bf16[128,256]{1,0:T(8,128)(2,1)} %x_in.1, bf16[128,4096]{1,0:T(8,128)(2,1)} %og_in.1, bf16[256,256]{1,0:T(8,128)(2,1)} %wq_in.1, bf16[256,256]{1,0:T(8,128)(2,1)} %wk_in.1, ...), custom_call_target="tpu_custom_call" | custom-call | tf_op jit(solution)/shard_map/pallas_call | solution.py:762
  167.0 1.5 shard_map.192
Async XLA Ops:
  1.3 0.7 copy-start

commit v4 on v3

--- a/solution.py
+++ b/solution.py
@@ -22,7 +22,7 @@
 
 
 def far_first(n):
-    return sorted(range(1, n), key=lambda d: (-min(d, n - d), d))
+    return sorted(range(1, n), key=lambda d: (min(d, n - d), d))
 
 
 def nn(a, b):
@@ -37,11 +37,11 @@
     tokens, depth = values.shape
     if tokens < TOK:
         values = jnp.concatenate([values, jnp.zeros((TOK - tokens, depth), values.dtype)], axis=0)
-    return nt(jnp.ones((8, depth), BF16), values.astype(BF16))
+    return nt(jnp.ones((8, depth), BF16), values.astype(BF16))[0:1]
 
 
 def as_columns(row):
-    return jnp.broadcast_to(row[0:1, :], (TOK, TOK)).T
+    return jnp.broadcast_to(row, (TOK, TOK)).T
 
 
 def widened(col, width):
@@ -286,7 +286,7 @@
             arrived(to_core[name])
 
     send_weights("qkvo")
-    len_all[y] = jnp.full((8, TOK), len_in[0], jnp.int32).astype(F32)
+    len_all[y] = jnp.full((1, TOK), len_in[0], jnp.int32).astype(F32)
     og_moved = [
         swapped(
             og_in.at[
@@ -450,7 +450,7 @@
         qkv_low[1, part, :] = (key_pre * scale_key).astype(BF16)
         qkv_low[2, part, :] = (value_pre * scale_value).astype(BF16)
     lane = lax.broadcasted_iota(jnp.int32, (TOK, TOK), 1)
-    real = lane.astype(F32) < len_all[nc * s_h + c][0:1, :]
+    real = lane.astype(F32) < len_all[nc * s_h + c]
     halves = [lane < HEAD_DIM, lane >= HEAD_DIM]
     zero = jnp.zeros((TOK, TOK), F32)
 
@@ -725,11 +725,11 @@
         buf(CUT, nz, PART, rows),
         buf(CUT, nz, PART, rows),
         buf(CUT, seqs * PART, wide),
-        buf(2, CUT, ny, 8, TOK, dtype=F32),
+        buf(2, CUT, ny, 1, TOK, dtype=F32),
         buf(2, CUT, TOK, TOK, dtype=F32),
         buf(nc, heads, TOK, TOK, dtype=F32),
         buf(nc, 1, extra, dtype=F32),
-        buf(ny, 8, TOK, dtype=F32),
+        buf(ny, 1, TOK, dtype=F32),
         buf(CUT, nc, seqs, PART, 3 * head_cols),
         buf(CUT, ny - 1, PART, 3 * head_cols),
         buf(2, TOK, head_cols, dtype=F32),
@@ -746,9 +746,9 @@
         buf(CUT, ny - 1, PART, ff_cols),
         buf(CUT, ny, PART, 2 * ff_cols),
         buf(CUT, ny, PART, ff_cols),
-        buf(2, CUT, ny, 8, TOK, dtype=F32),
-        buf(2, CUT, seqs, 8, TOK, dtype=F32),
-        buf(2, CUT, nz - 1, 8, TOK, dtype=F32),
+        buf(2, CUT, ny, 1, TOK, dtype=F32),
+        buf(2, CUT, seqs, 1, TOK, dtype=F32),
+        buf(2, CUT, nz - 1, 1, TOK, dtype=F32),
         buf(CUT, PART, rows, dtype=F32),
         buf(CUT, nz, PART, rows),
         buf(CUT, nc, seqs, PART, head_cols),

time: 169 us -> 163 us (0.964)
  Pallas kernels: 166 us -> 160 us
    pallas_call x1, Pallas kernels: 164 us -> 158 us  [on_device(): pl.pallas_call(functools.partial(layer_kernel, sizes), out_shape=(jax.Sha...]
where the time goes in v4:
time: 163 us; the launch traced here: 162 us
  Pallas kernels  160 us (98%)
    pallas_call x1, Pallas kernels, on_device(): pl.pallas_call(functools.partial(layer_kernel, sizes), out_shape=(jax.Sha...  158 us

profile of v4, /device:TPU:33, one launch (start us, length us, event | category | flops | bytes accessed | tf_op | source)
XLA Modules:
  0.0 162.2 jit_solution(13587765771751642652)
XLA Ops:
  1.3 0.0 copy-start
  1.3 0.7 copy-done
  2.0 0.6 broadcast_in_dim.11.sf_in
  2.5 158.1 %shard_map.191 = (bf16[128,256]{1,0:T(8,128)(2,1)}, bf16[128,256]{1,0:T(8,128)(2,1)}, f32[1,256]{1,0:T(1,128)}, f32[1,256]{1,0:T(1,128)}, f32[1,640]{1,0:T(1,128)}) custom-call(bf16[128,256]{1,0:T(8,128)(2,1)} %x_in.1, bf16[128,4096]{1,0:T(8,128)(2,1)} %og_in.1, bf16[256,256]{1,0:T(8,128)(2,1)} %wq_in.1, bf16[256,256]{1,0:T(8,128)(2,1)} %wk_in.1, ...), custom_call_target="tpu_custom_call" | custom-call | tf_op jit(solution)/shard_map/pallas_call | solution.py:762
  160.7 1.5 shard_map.192
Async XLA Ops:
  1.3 0.7 copy-start

commit v5 on v4

--- a/solution.py
+++ b/solution.py
@@ -285,7 +285,7 @@
             own_w[name].wait()
             arrived(to_core[name])
 
-    send_weights("qkvo")
+    send_weights("qkv")
     len_all[y] = jnp.full((1, TOK), len_in[0], jnp.int32).astype(F32)
     og_moved = [
         swapped(
@@ -310,8 +310,8 @@
     for h in cuts:
         x_moved[h]()
         x_gathered.append(links.share(ZA, gx.at[h, z]))
-    relay("qkvo")
-    send_weights("dgu")
+    relay("qkv")
+    send_weights("o")
 
     def stacked(blocks, a):
         return jnp.concatenate([blocks[seqs * a + s] for s in range(seqs)], axis=0)
@@ -421,6 +421,8 @@
         arrived(x_gathered[h])
         sq1.append(normed(0, h, gx.at[h], norm_a))
     relay_far("qkv")
+    relay("o")
+    send_weights("dgu")
     weights_ready("qkv")
     moved = [scatter_y(h, gn[h], wqkv, sb_qkv, rb_qkv) for h in cuts]
     og_gathered = []
@@ -626,29 +628,31 @@
         dqkv_gathered.append(links.share(YA, gdqkv.at[h, y]))
 
     gv_c = links.share(CA, gv.at[0, 0], gv.at[0, 1])
-    out_moved = []
-    for h in cuts:
-        arrived(ff_moved[h])
-        tout[0, h] = (fs_r[h] + total_z(2, h)).astype(BF16)
-        out_moved.append(swapped(tout.at[0, h], tout.at[2, h]))
-    arrived(gv_c)
-    total = gv[0, 0]
-    if nc > 1:
-        total = total + gv[0, 1]
-    gv[1, y] = total
-    gv_y = links.share(YA, gv.at[1, y])
     moved = []
     for h in cuts:
         arrived(dot_gathered[h])
         chip_sums(1, h)
         arrived(dqkv_gathered[h])
         moved.append(scatter_z(3, h, gdqkv, wqkv, 1))
-    arrived(gv_y)
-    total = gv[1, c]
-    for s in range(1, seqs):
-        total = total + gv[1, nc * s + c]
-    gv[2, x] = total
-    gv_x = links.share(XA, gv.at[2, x])
+        if h == 0:
+            arrived(gv_c)
+            total = gv[0, 0]
+            if nc > 1:
+                total = total + gv[0, 1]
+            gv[1, y] = total
+            gv_y = links.share(YA, gv.at[1, y])
+        if h == CUT - 1:
+            arrived(gv_y)
+            total = gv[1, c]
+            for s in range(1, seqs):
+                total = total + gv[1, nc * s + c]
+            gv[2, x] = total
+            gv_x = links.share(XA, gv.at[2, x])
+    out_moved = []
+    for h in cuts:
+        arrived(ff_moved[h])
+        tout[0, h] = (fs_r[h] + total_z(2, h)).astype(BF16)
+        out_moved.append(swapped(tout.at[0, h], tout.at[2, h]))
     ig_moved = []
     for h in cuts:
         inv_first = inverse(0, h, s_r, rows)

time: 163 us -> 162 us (level)
  no operation moved by 1% of the time
where the time goes in v5:
time: 162 us
  Pallas kernels  159 us (98%)
    pallas_call x1, Pallas kernels, on_device(): pl.pallas_call(functools.partial(layer_kernel, sizes), out_shape=(jax.Sha...  158 us

profile of v5, /device:TPU:33, one launch (start us, length us, event | category | flops | bytes accessed | tf_op | source)
XLA Modules:
  0.0 161.8 jit_solution(3799562068137726485)
XLA Ops:
  1.3 0.0 copy-start
  1.3 0.7 copy-done
  2.0 0.6 broadcast_in_dim.11.sf_in
  2.5 157.7 %shard_map.191 = (bf16[128,256]{1,0:T(8,128)(2,1)}, bf16[128,256]{1,0:T(8,128)(2,1)}, f32[1,256]{1,0:T(1,128)}, f32[1,256]{1,0:T(1,128)}, f32[1,640]{1,0:T(1,128)}) custom-call(bf16[128,256]{1,0:T(8,128)(2,1)} %x_in.1, bf16[128,4096]{1,0:T(8,128)(2,1)} %og_in.1, bf16[256,256]{1,0:T(8,128)(2,1)} %wq_in.1, bf16[256,256]{1,0:T(8,128)(2,1)} %wk_in.1, ...), custom_call_target="tpu_custom_call" | custom-call | tf_op jit(solution)/shard_map/pallas_call | solution.py:766
  160.2 1.5 shard_map.192
Async XLA Ops:
  1.3 0.7 copy-start
